TPU v7x, 32 devices: a whole 2x2x4 slice. The times are simulated.
32 devices in a mesh: gx: 4 (over y, x), gy: 2 (over core), row: 4 (over z).
Axes of the slice: x: 2, y: 2, z: 4, core: 2. Of those that a mesh axis runs over, the one named last changes fastest.
Arguments:
- occupancy: int32 [32, 512, 1024], P('row', 'gx', 'gy'), may hold values 0 or 1
- random_draws: bfloat16 [4, 32, 512, 1024], P(None, 'row', 'gx', 'gy'), may hold values from 0 to 1
Outputs:
- coverage: float32 [128, 256], P('gx', 'gy')
- projected: float32 [128, 256], P('gx', 'gy')
All inputs are finite; a program needn't handle non-finite values. No bound on the sum of `occupancy` on one device may be relied on, other than what follows from the above.
Results may differ from a plain program's by a relative error of at most 0.0003.
Values may be sent and summed in bfloat16 or wider, within the bound.
No kernel may reach another device: no remote copies, remote signals or barrier semaphores. Data moves between devices by JAX's collectives and lax.ppermute only.
A program may use at most 64 MiB of HBM per device.

v0:
```python
import jax
import jax.numpy as jnp
from jax import lax
from jax.sharding import PartitionSpec as P

SWEEPS = 4
BLOCK = 4
LEAP = 8


ADSORB = 0.6
DESORB = 0.6
HOPPING = 0.3
COUPLING = 0.5


def padded_2(block, sides, width):
    for axis, dim in sides:
        count = lax.axis_size(axis)
        forward = [(i, i + 1) for i in range(count - 1)]
        forward.append((count - 1, 0))
        backward = [(target, source) for source, target in forward]
        low = lax.ppermute(
            lax.slice_in_dim(block, block.shape[dim] - width, None, axis=dim), axis, forward
        )
        high = lax.ppermute(lax.slice_in_dim(block, 0, width, axis=dim), axis, backward)
        block = jnp.concatenate([low, block, high], axis=dim)
    return block


def sublattice_update(padded, jitter, colour):
    centre = padded[..., 1:-1, 1:-1]
    beside = (
        padded[..., 2:, 1:-1]
        + padded[..., :-2, 1:-1]
        + padded[..., 1:-1, 2:]
        + padded[..., 1:-1, :-2]
    )
    updated = (
        centre
        + ADSORB * jitter * (1.0 - centre)
        - DESORB * (1.0 - jitter) * jnp.exp(-COUPLING * beside) * centre
        + HOPPING * (0.25 * beside - centre)
    )
    row_index = lax.broadcasted_iota(jnp.int32, centre.shape[-2:], 0)
    col_index = lax.broadcasted_iota(jnp.int32, centre.shape[-2:], 1)
    chosen = (row_index + col_index + colour) % 2 == 0
    return jnp.where(chosen[None], updated, centre)


def block_sums(field):
    height, width = (field.shape[-2], field.shape[-1])
    shaped = field.reshape(field.shape[:-2] + (height // BLOCK, BLOCK, width // BLOCK, BLOCK))
    return jnp.sum(shaped, axis=(-3, -1))


def per_device(occupancy, random_draws):
    occupied = occupancy.astype(jnp.float32)
    earlier = occupied
    even_draws = padded_2(random_draws[0::2], (("gx", 2), ("gy", 3)), 1)
    for pair_index in range(SWEEPS // 2):
        if 2 * pair_index == SWEEPS - 2:
            earlier = occupied
        widened = padded_2(occupied, (("gx", 1), ("gy", 2)), 2)
        middle = sublattice_update(widened, even_draws[pair_index].astype(jnp.float32), 0)
        occupied = sublattice_update(
            middle, random_draws[2 * pair_index + 1].astype(jnp.float32), 1
        )
    snapshots = jnp.stack([jnp.sum(earlier, axis=0), jnp.sum(occupied, axis=0)])
    coarse_sums = lax.psum(block_sums(snapshots), "row")
    divisor = jnp.float32(occupancy.shape[0] * lax.axis_size("row") * BLOCK * BLOCK)
    averages = coarse_sums / divisor
    coverage = averages[1]
    projected = coverage + LEAP / 2.0 * (coverage - averages[0])
    return (coverage, projected)


def solution(mesh):
    in_specs = (P("row", "gx", "gy"), P(None, "row", "gx", "gy"))
    out_specs = (P("gx", "gy"), P("gx", "gy"))
    return jax.shard_map(
        per_device, mesh=mesh, in_specs=in_specs, out_specs=out_specs, check_vma=False
    )
```

profile of v0, /device:TPU:0, one launch (start us, length us, event | category | flops | bytes accessed | tf_op | source)
XLA Modules:
  0.0 108.9 jit_solution(14045809891136270607)
XLA Ops:
  0.6 3.0 %copy_convert_fusion = f32[8,128,512]{2,0,1:T(8,128)S(1)} fusion(s32[8,128,512]{2,1,0:T(8,128)} %param.2), kind=kLoop, calls=%fused_computation.76 | loop fusion | flops 524288 | bytes 4194304 | tf_op jit(solution)/shard_map/convert_element_type | solution.py:58
  3.6 3.0 %collective-permute-start = (f32[8,2,512]{2,0,1:T(8,128)S(1)}, f32[8,2,512]{2,0,1:T(8,128)S(1)}, u32[]{:S(2)}, u32[]{:S(2)}) collective-permute-start(f32[8,2,512]{2,0,1:T(8,128)S(1)} %get-tuple-element.18), channel_id=1, source_target_pairs={{0,8},{8,16},{16,24},{24,0},{1,9},{9,17},{17,25},{25,1},{2,10},{10... | collective-permute-start | bytes 98312 | tf_op jit(solution)/shard_map/ppermute | solution.py:23
  6.6 1.0 collective-permute-start.1
  7.7 0.2 slice.126
  7.9 1.1 collective-permute-start.4
  9.0 1.9 %collective-permute-start.5 = (bf16[2,8,1,512]{3,1,2,0:T(8,128)(2,1)S(1)}, bf16[2,8,1,512]{3,1,2,0:T(8,128)(2,1)S(1)}, u32[]{:S(2)}, u32[]{:S(2)}) collective-permute-start(bf16[2,8,1,512]{3,1,2,0:T(8,128)(2,1)S(1)} %copy.54), channel_id=1, source_target_pairs={{8,0},{16,8},{24,16},{0,24},{9,1},{17,9},{25,17},{1,25},{10,2},{18... | collective-permute-start | bytes 49160 | tf_op jit(solution)/shard_map/ppermute | solution.py:26
  10.9 1.5 %fusion.57 = (bf16[1,8,128,512]{3,2,1,0:T(8,128)(2,1)}, bf16[1,8,128,512]{3,2,1,0:T(8,128)(2,1)}) fusion(bf16[4,8,128,512]{3,2,1,0:T(8,128)(2,1)S(1)} %copy-done.3), kind=kLoop, calls=%fused_computation.107 | loop fusion | bytes 4194304 | tf_op jit(solution)/shard_map/slice | solution.py:67
  12.5 0.1 collective-permute-done.4
  12.6 1.2 %constant_dynamic-update-slice_fusion.1 = bf16[2,8,130,512]{3,1,2,0:T(8,128)(2,1)S(1)} fusion(bf16[2,8,130,512]{3,1,2,0:T(8,128)(2,1)S(1)} %constant_dynamic-update-slice_fusion.2, bf16[2,8,128,512]{3,2,1,0:T(8,128)(2,1)S(1)} %slice.126), kind=kLoop, calls=%fused_computation.104 | loop fusion | bytes 4194304
  13.8 1.3 %copy-done.2 = bf16[2,8,130,512]{3,1,2,0:T(8,128)(2,1)} copy-done((bf16[2,8,130,512]{3,1,2,0:T(8,128)(2,1)}, bf16[2,8,130,512]{3,1,2,0:T(8,128)(2,1)S(1)}, u32[]{:S(2)}) %copy-start.2) | copy-done | bytes 2129944
  15.1 0.3 fusion.58
  15.4 0.4 copy.16
  15.9 0.4 copy.17
  16.3 0.5 collective-permute-start.7
  16.9 0.7 fusion.51
  17.6 1.3 %copy.18 = bf16[2,8,130,1]{3,1,2,0:T(8,128)(2,1)} copy(bf16[2,8,130,1]{2,1,3,0:T(8,128)(2,1)S(1)} %collective-permute-done.6) | data formatting | bytes 8320 | tf_op jit(solution)/shard_map/ppermute | solution.py:23
  18.9 1.3 %copy.19 = bf16[2,8,130,1]{3,1,2,0:T(8,128)(2,1)} copy(bf16[2,8,130,1]{2,1,3,0:T(8,128)(2,1)S(1)} %collective-permute-done.7) | data formatting | bytes 8320 | tf_op jit(solution)/shard_map/ppermute | solution.py:26
  20.2 0.2 pad_maximum_fusion.18
  20.4 0.3 copy.11
  20.8 0.3 copy.12
  21.1 0.5 collective-permute-start.3
  21.6 5.0 %pad_maximum_fusion.14 = bf16[2,8,130,514]{3,1,2,0:T(8,128)(2,1)} fusion(bf16[2,8,130,1]{3,1,2,0:T(8,128)(2,1)} %copy.19, bf16[2,8,130,512]{3,1,2,0:T(8,128)(2,1)} %copy-done.2, bf16[2,8,130,1]{3,1,2,0:T(8,128)(2,1)} %copy.18), kind=kLoop, calls=%fused_computation.44 | loop fusion | flops 6414720 | bytes 4276480 | tf_op jit(solution)/shard_map/concatenate | solution.py:27
  26.7 0.4 copy.13
  27.1 0.4 copy.14
  27.5 0.9 pad_maximum_fusion
  28.4 0.8 copy-done
  29.2 4.2 %fusion.5 = f32[8,130,514]{2,0,1:T(8,128)S(1)} fusion(f32[8,2,512]{2,0,1:T(8,128)S(1)} %collective-permute-done.1, f32[8,128,512]{2,0,1:T(8,128)S(1)} %copy_convert_fusion, f32[8,2,512]{2,0,1:T(8,128)S(1)} %collective-permute-done, f32[8,132,2]{2,0,1:T(8,128)S(1)} %copy.13, f32[8,132,2]{2,0,1:T(8,128)S(1)} %copy.14, f32[8,132,516]{2,0,1:T(8,128)S(1)} %pad_maximum_fusion, ...), kind=kLoop, calls=%fused_computation.11 | loop fusion | flops 13364000 | bytes 11868484 | tf_op jit(solution)/shard_map/jit(_where)/select_n | solution.py:48
  33.5 4.6 %fusion.55 = (f32[128,512]{1,0:T(8,128)S(1)}, f32[8,128,512]{2,0,1:T(8,128)S(1)}) fusion(f32[8,130,514]{2,0,1:T(8,128)S(1)} %fusion.5, bf16[1,8,128,512]{3,2,1,0:T(8,128)(2,1)S(1)} %copy-done.5, pred[128,512]{1,0:T(8,128)(4,1)S(1)} %copy-done.6), kind=kLoop, calls=%fused_computation.106 | loop fusion | flops 10420224 | bytes 13959168 | tf_op jit(solution)/shard_map/reduce_sum | solution.py:69
  38.1 2.3 %collective-permute-start.8 = (f32[8,2,512]{2,0,1:T(8,128)S(1)}, f32[8,2,512]{2,0,1:T(8,128)S(1)}, u32[]{:S(2)}, u32[]{:S(2)}) collective-permute-start(f32[8,2,512]{2,0,1:T(8,128)S(1)} %get-tuple-element.14), channel_id=1, source_target_pairs={{0,8},{8,16},{16,24},{24,0},{1,9},{9,17},{17,25},{25,1},{2,10},{10... | collective-permute-start | bytes 98312 | tf_op jit(solution)/shard_map/ppermute | solution.py:23
  40.3 0.7 collective-permute-start.9
  41.1 2.0 %collective-permute-done.8 = f32[8,2,512]{2,0,1:T(8,128)S(1)} collective-permute-done((f32[8,2,512]{2,0,1:T(8,128)S(1)}, f32[8,2,512]{2,0,1:T(8,128)S(1)}, u32[]{:S(2)}, u32[]{:S(2)}) %collective-permute-start.8) | collective-permute-done | bytes 32800 | tf_op jit(solution)/shard_map/ppermute | solution.py:23
  43.1 1.2 %collective-permute-done.9 = f32[8,2,512]{2,0,1:T(8,128)S(1)} collective-permute-done((f32[8,2,512]{2,0,1:T(8,128)S(1)}, f32[8,2,512]{2,0,1:T(8,128)S(1)}, u32[]{:S(2)}, u32[]{:S(2)}) %collective-permute-start.9) | collective-permute-done | bytes 32800 | tf_op jit(solution)/shard_map/ppermute | solution.py:26
  44.3 0.2 pad_maximum_fusion.15
  44.5 0.4 copy-done.10
  44.9 0.3 copy.25
  45.3 0.3 copy.26
  45.6 0.5 collective-permute-start.11
  46.2 10.0 %reshape.78 = f32[1,32,4,128,4]{4,3,2,1,0:T(8,128)} reshape(f32[128,512]{1,0:T(8,128)S(1)} %get-tuple-element.4) | data formatting | bytes 524288 | tf_op jit(solution)/shard_map/stack | solution.py:69
  56.2 5.2 %copy.34 = f32[1,32,4,128,4]{3,1,4,2,0:T(8,128)S(1)} copy(f32[1,32,4,128,4]{4,3,2,1,0:T(8,128)} %reshape.78) | data formatting | bytes 524288 | tf_op jit(solution)/shard_map/stack | solution.py:69
  61.5 0.4 copy.27
  61.9 1.1 %copy.28 = f32[8,132,2]{2,0,1:T(8,128)S(1)} copy(f32[8,132,2]{1,0,2:T(8,128)} %collective-permute-done.11) | data formatting | bytes 16896 | tf_op jit(solution)/shard_map/ppermute | solution.py:26
  63.0 1.8 %pad_maximum_fusion.1 = f32[8,132,516]{2,0,1:T(8,128)S(1)} fusion(f32[8,132,2]{2,0,1:T(8,128)S(1)} %copy.28, f32[8,2,512]{2,0,1:T(8,128)} %copy-done.10, f32[8,128,512]{2,0,1:T(8,128)S(1)} %get-tuple-element.5, f32[8,2,512]{2,0,1:T(8,128)} %copy-done.8, f32[8,132,2]{2,0,1:T(8,128)S(1)} %copy.27), kind=kLoop, calls=%fused_computation.5 | loop fusion | flops 2179584 | bytes 4359168 | tf_op jit(solution)/shard_map/concatenate | solution.py:27
  64.9 4.2 %fusion.15 = f32[8,130,514]{2,0,1:T(8,128)S(1)} fusion(f32[8,2,512]{2,0,1:T(8,128)S(1)} %copy-done.11, f32[8,128,512]{2,0,1:T(8,128)S(1)} %get-tuple-element.5, f32[8,2,512]{2,0,1:T(8,128)S(1)} %copy-done.9, f32[8,132,2]{2,0,1:T(8,128)S(1)} %copy.27, f32[8,132,2]{2,0,1:T(8,128)S(1)} %copy.28, f32[8,132,516]{2,0,1:T(8,128)S(1)} %pad_maximum_fusion.1, ...), kind=kLoop, calls=%fused_computation.21 | loop fusion | flops 13364000 | bytes 11868484 | tf_op jit(solution)/shard_map/jit(_where)/select_n | solution.py:48
  69.2 4.5 %fusion.40 = f32[128,512]{1,0:T(8,128)S(1)} fusion(f32[8,130,514]{2,0,1:T(8,128)S(1)} %fusion.15, bf16[1,8,128,512]{3,2,1,0:T(8,128)(2,1)S(1)} %copy-done.4, pred[128,512]{1,0:T(8,128)(4,1)S(1)} %copy-done.7), kind=kLoop, calls=%fused_computation.65 | loop fusion | flops 10420224 | bytes 11862016 | tf_op jit(solution)/shard_map/reduce_sum | solution.py:69
  73.7 10.0 %reshape.79 = f32[1,32,4,128,4]{4,3,2,1,0:T(8,128)} reshape(f32[128,512]{1,0:T(8,128)S(1)} %fusion.40) | data formatting | bytes 524288 | tf_op jit(solution)/shard_map/stack | solution.py:69
  83.7 5.2 %copy.35 = f32[1,32,4,128,4]{3,1,4,2,0:T(8,128)S(1)} copy(f32[1,32,4,128,4]{4,3,2,1,0:T(8,128)} %reshape.79) | data formatting | bytes 524288 | tf_op jit(solution)/shard_map/stack | solution.py:69
  89.0 19.3 %psum.7 = f32[2,32,128]{2,1,0:T(8,128)S(1)} all-reduce(f32[2,32,128]{2,1,0:T(8,128)S(1)} %maximum_reduce_fusion), channel_id=1, replica_groups=mesh['gx'=4,'gy'=2,'row'=4] {'row'}, use_global_device_ids=true, to_apply=%region_3.4 | all-reduce | flops 8192 | bytes 65536 | tf_op jit(solution)/shard_map/psum | solution.py:70
  108.3 0.6 fusion.54
  (43 shorter events, 0.4 us)
Async XLA Ops:
  0.6 7.0 %copy-start.3 = (bf16[4,8,128,512]{3,2,1,0:T(8,128)(2,1)S(1)}, bf16[4,8,128,512]{3,2,1,0:T(8,128)(2,1)}, u32[]{:S(2)}) copy-start(bf16[4,8,128,512]{3,2,1,0:T(8,128)(2,1)} %param.3) | copy-start | bytes 12582916
  3.6 16.5 %collective-permute-start = (f32[8,2,512]{2,0,1:T(8,128)S(1)}, f32[8,2,512]{2,0,1:T(8,128)S(1)}, u32[]{:S(2)}, u32[]{:S(2)}) collective-permute-start(f32[8,2,512]{2,0,1:T(8,128)S(1)} %get-tuple-element.18), channel_id=1, source_target_pairs={{0,8},{8,16},{16,24},{24,0},{1,9},{9,17},{17,25},{25,1},{2,10},{10... | collective-permute-start | bytes 98312 | tf_op jit(solution)/shard_map/ppermute | solution.py:23
  6.6 13.5 %collective-permute-start.1 = (f32[8,2,512]{2,0,1:T(8,128)S(1)}, f32[8,2,512]{2,0,1:T(8,128)S(1)}, u32[]{:S(2)}, u32[]{:S(2)}) collective-permute-start(f32[8,2,512]{2,0,1:T(8,128)S(1)} %get-tuple-element.19), channel_id=1, source_target_pairs={{8,0},{16,8},{24,16},{0,24},{9,1},{17,9},{25,17},{1,25},{10,2},{18... | collective-permute-start | bytes 98312 | tf_op jit(solution)/shard_map/ppermute | solution.py:26
  7.9 4.7 %collective-permute-start.4 = (bf16[2,8,1,512]{3,1,2,0:T(8,128)(2,1)S(1)}, bf16[2,8,1,512]{3,1,2,0:T(8,128)(2,1)S(1)}, u32[]{:S(2)}, u32[]{:S(2)}) collective-permute-start(bf16[2,8,1,512]{3,1,2,0:T(8,128)(2,1)S(1)} %copy.53), channel_id=1, source_target_pairs={{0,8},{8,16},{16,24},{24,0},{1,9},{9,17},{17,25},{25,1},{2,10},{10... | collective-permute-start | bytes 49160 | tf_op jit(solution)/shard_map/ppermute | solution.py:23
  9.0 4.8 %collective-permute-start.5 = (bf16[2,8,1,512]{3,1,2,0:T(8,128)(2,1)S(1)}, bf16[2,8,1,512]{3,1,2,0:T(8,128)(2,1)S(1)}, u32[]{:S(2)}, u32[]{:S(2)}) collective-permute-start(bf16[2,8,1,512]{3,1,2,0:T(8,128)(2,1)S(1)} %copy.54), channel_id=1, source_target_pairs={{8,0},{16,8},{24,16},{0,24},{9,1},{17,9},{25,17},{1,25},{10,2},{18... | collective-permute-start | bytes 49160 | tf_op jit(solution)/shard_map/ppermute | solution.py:26
  13.8 1.3 %copy-start.2 = (bf16[2,8,130,512]{3,1,2,0:T(8,128)(2,1)}, bf16[2,8,130,512]{3,1,2,0:T(8,128)(2,1)S(1)}, u32[]{:S(2)}) copy-start(bf16[2,8,130,512]{3,1,2,0:T(8,128)(2,1)S(1)} %constant_dynamic-update-slice_fusion) | copy-start | bytes 6389764
  15.8 1.8 %collective-permute-start.6 = (bf16[2,8,130,1]{2,1,3,0:T(8,128)(2,1)S(1)}, bf16[2,8,130,1]{2,1,3,0:T(8,128)(2,1)S(1)}, u32[]{:S(2)}, u32[]{:S(2)}) collective-permute-start(bf16[2,8,130,1]{2,1,3,0:T(8,128)(2,1)S(1)} %copy.16), channel_id=1, source_target_pairs={{0,4},{4,0},{1,5},{5,1},{2,6},{6,2},{3,7},{7,3},{8,12},{12,8},{9,1... | collective-permute-start | bytes 12488 | tf_op jit(solution)/shard_map/ppermute | solution.py:23
  16.3 2.5 %collective-permute-start.7 = (bf16[2,8,130,1]{2,1,3,0:T(8,128)(2,1)S(1)}, bf16[2,8,130,1]{2,1,3,0:T(8,128)(2,1)S(1)}, u32[]{:S(2)}, u32[]{:S(2)}) collective-permute-start(bf16[2,8,130,1]{2,1,3,0:T(8,128)(2,1)S(1)} %copy.17), channel_id=1, source_target_pairs={{4,0},{0,4},{5,1},{1,5},{6,2},{2,6},{7,3},{3,7},{12,8},{8,12},{13,... | collective-permute-start | bytes 12488 | tf_op jit(solution)/shard_map/ppermute | solution.py:26
  20.7 6.0 %collective-permute-start.2 = (f32[8,132,2]{1,0,2:T(8,128)S(1)}, f32[8,132,2]{1,0,2:T(8,128)S(1)}, u32[]{:S(2)}, u32[]{:S(2)}) collective-permute-start(f32[8,132,2]{1,0,2:T(8,128)S(1)} %copy.11), channel_id=1, source_target_pairs={{0,4},{4,0},{1,5},{5,1},{2,6},{6,2},{3,7},{7,3},{8,12},{12,8},{9,1... | collective-permute-start | bytes 25352 | tf_op jit(solution)/shard_map/ppermute | solution.py:23
  21.1 6.0 %collective-permute-start.3 = (f32[8,132,2]{1,0,2:T(8,128)S(1)}, f32[8,132,2]{1,0,2:T(8,128)S(1)}, u32[]{:S(2)}, u32[]{:S(2)}) collective-permute-start(f32[8,132,2]{1,0,2:T(8,128)S(1)} %copy.12), channel_id=1, source_target_pairs={{4,0},{0,4},{5,1},{1,5},{6,2},{2,6},{7,3},{3,7},{12,8},{8,12},{13,... | collective-permute-start | bytes 25352 | tf_op jit(solution)/shard_map/ppermute | solution.py:26
  27.5 1.8 %copy-start = (bf16[2,8,130,514]{3,1,2,0:T(8,128)(2,1)S(1)}, bf16[2,8,130,514]{3,1,2,0:T(8,128)(2,1)}, u32[]{:S(2)}) copy-start(bf16[2,8,130,514]{3,1,2,0:T(8,128)(2,1)} %pad_maximum_fusion.14) | copy-start | bytes 6414724
  29.2 4.2 %copy-start.5 = (bf16[1,8,128,512]{3,2,1,0:T(8,128)(2,1)S(1)}, bf16[1,8,128,512]{3,2,1,0:T(8,128)(2,1)}, u32[]{:S(2)}) copy-start(bf16[1,8,128,512]{3,2,1,0:T(8,128)(2,1)} %get-tuple-element.7) | copy-start | bytes 3145732
  29.2 4.2 %copy-start.6 = (pred[128,512]{1,0:T(8,128)(4,1)S(1)}, pred[128,512]{1,0:T(8,128)(4,1)}, u32[]{:S(2)}) copy-start(pred[128,512]{1,0:T(8,128)(4,1)} %fusion.51) | copy-start | bytes 196612
  38.1 5.0 %collective-permute-start.8 = (f32[8,2,512]{2,0,1:T(8,128)S(1)}, f32[8,2,512]{2,0,1:T(8,128)S(1)}, u32[]{:S(2)}, u32[]{:S(2)}) collective-permute-start(f32[8,2,512]{2,0,1:T(8,128)S(1)} %get-tuple-element.14), channel_id=1, source_target_pairs={{0,8},{8,16},{16,24},{24,0},{1,9},{9,17},{17,25},{25,1},{2,10},{10... | collective-permute-start | bytes 98312 | tf_op jit(solution)/shard_map/ppermute | solution.py:23
  40.3 3.9 %collective-permute-start.9 = (f32[8,2,512]{2,0,1:T(8,128)S(1)}, f32[8,2,512]{2,0,1:T(8,128)S(1)}, u32[]{:S(2)}, u32[]{:S(2)}) collective-permute-start(f32[8,2,512]{2,0,1:T(8,128)S(1)} %get-tuple-element.15), channel_id=1, source_target_pairs={{8,0},{16,8},{24,16},{0,24},{9,1},{17,9},{25,17},{1,25},{10,2},{18... | collective-permute-start | bytes 98312 | tf_op jit(solution)/shard_map/ppermute | solution.py:26
  43.1 1.2 %copy-start.8 = (f32[8,2,512]{2,0,1:T(8,128)}, f32[8,2,512]{2,0,1:T(8,128)S(1)}, u32[]{:S(2)}) copy-start(f32[8,2,512]{2,0,1:T(8,128)S(1)} %collective-permute-done.8) | copy-start | bytes 98308
  44.3 0.6 copy-start.10
  45.2 16.2 %collective-permute-start.10 = (f32[8,132,2]{1,0,2:T(8,128)S(1)}, f32[8,132,2]{1,0,2:T(8,128)S(1)}, u32[]{:S(2)}, u32[]{:S(2)}) collective-permute-start(f32[8,132,2]{1,0,2:T(8,128)S(1)} %copy.25), channel_id=1, source_target_pairs={{0,4},{4,0},{1,5},{5,1},{2,6},{6,2},{3,7},{7,3},{8,12},{12,8},{9,1... | collective-permute-start | bytes 25352 | tf_op jit(solution)/shard_map/ppermute | solution.py:23
  45.6 16.2 %collective-permute-start.11 = (f32[8,132,2]{1,0,2:T(8,128)S(1)}, f32[8,132,2]{1,0,2:T(8,128)}, u32[]{:S(2)}, u32[]{:S(2)}) collective-permute-start(f32[8,132,2]{1,0,2:T(8,128)S(1)} %copy.26), channel_id=1, source_target_pairs={{4,0},{0,4},{5,1},{1,5},{6,2},{2,6},{7,3},{3,7},{12,8},{8,12},{13,... | collective-permute-start | bytes 25352 | tf_op jit(solution)/shard_map/ppermute | solution.py:26
  63.0 1.9 %copy-start.1 = (bf16[2,8,130,514]{3,1,2,0:T(8,128)(2,1)S(1)}, bf16[2,8,130,514]{3,1,2,0:T(8,128)(2,1)}, u32[]{:S(2)}) copy-start(bf16[2,8,130,514]{3,1,2,0:T(8,128)(2,1)} %pad_maximum_fusion.14) | copy-start | bytes 6414724
  63.0 1.9 %copy-start.9 = (f32[8,2,512]{2,0,1:T(8,128)S(1)}, f32[8,2,512]{2,0,1:T(8,128)}, u32[]{:S(2)}) copy-start(f32[8,2,512]{2,0,1:T(8,128)} %copy-done.8) | copy-start | bytes 98308
  63.0 1.9 %copy-start.11 = (f32[8,2,512]{2,0,1:T(8,128)S(1)}, f32[8,2,512]{2,0,1:T(8,128)}, u32[]{:S(2)}) copy-start(f32[8,2,512]{2,0,1:T(8,128)} %copy-done.10) | copy-start | bytes 98308
  64.9 4.3 %copy-start.4 = (bf16[1,8,128,512]{3,2,1,0:T(8,128)(2,1)S(1)}, bf16[1,8,128,512]{3,2,1,0:T(8,128)(2,1)}, u32[]{:S(2)}) copy-start(bf16[1,8,128,512]{3,2,1,0:T(8,128)(2,1)} %get-tuple-element.6) | copy-start | bytes 3145732
  64.9 4.3 %copy-start.7 = (pred[128,512]{1,0:T(8,128)(4,1)S(1)}, pred[128,512]{1,0:T(8,128)(4,1)}, u32[]{:S(2)}) copy-start(pred[128,512]{1,0:T(8,128)(4,1)} %fusion.51) | copy-start | bytes 196612
where the time goes:
time: 109 us
  local copies, waits for them, and re-layouts  43.4 us (40%)
  other arithmetic  30.1 us (28%)
  blocking collectives  19.3 us (18%)
  starting transfers between devices  11.8 us (11%)
  waiting for transfers between devices  3.33 us (3%)
    another operation x4, local copies, waits for them, and re-layouts, per_device(): snapshots = jnp.stack([jnp.sum(earlier, axis=0), jnp.sum(occupied, axis=0)])  30.5 us
    psum x1, blocking collectives, per_device(): coarse_sums = lax.psum(block_sums(snapshots), 'row')  19.3 us
    reduce_sum x2, other arithmetic, per_device(): snapshots = jnp.stack([jnp.sum(earlier, axis=0), jnp.sum(occupied, axis=0)])  9.11 us
    select_n x2, other arithmetic, sublattice_update(): return jnp.where(chosen[None], updated, centre)  8.46 us
    concatenate x5, other arithmetic, padded_2(): block = jnp.concatenate([low, block, high], axis=dim)  8.14 us
    ppermute x6, starting transfers between devices, padded_2(): lax.ppermute(lax.slice_in_dim(block, block.shape[dim] - width, None, axis...  6.51 us
    ppermute x6, starting transfers between devices, padded_2(): lax.ppermute(lax.slice_in_dim(block, 0, width, axis=dim), axis, backward)  5.3 us
    unnamed x28, local copies, waits for them, and re-layouts  3.81 us
  transfers between devices with their start and end apart: 12, of which 3 were waited for; matrix products, arithmetic and copies ran while one was open for 27% of the time, Pallas kernels for 0%

commit v1 on v0

v1 whole, which is shorter than its diff:
```python
import functools
import math

import jax
import jax.numpy as jnp
from jax import lax
from jax.experimental import pallas as pl
from jax.experimental.pallas import tpu as pltpu
from jax.sharding import PartitionSpec as P

SWEEPS = 4
BLOCK = 4
LEAP = 8

ADSORB = 0.6
DESORB = 0.6
HOPPING = 0.3
COUPLING = 0.5

LANES = 128
GROUP = 16
F32 = jnp.float32
BF16 = jnp.bfloat16
MIB = 1 << 20


def iota(shape, dim):
    return lax.broadcasted_iota(jnp.int32, shape, dim)


def even_lanes(shape):
    return iota(shape, len(shape) - 1) % 2 == 0


def updated(centre, beside, draw):
    gone = 1.0 - jnp.exp2(beside * (-COUPLING * math.log2(math.e)))
    gain = ADSORB * draw
    keep = (1.0 - HOPPING - ADSORB) + (ADSORB - gain) * gone
    return centre * keep + (gain + (0.25 * HOPPING) * beside)


def fold_lanes(width, first, rows_per=1):
    source = iota((width, LANES), 0)
    target = iota((width, LANES), 1)
    return jnp.where(source // BLOCK + first == target, 1.0, 0.0).astype(F32)


def exact_dot(a, b):
    return jnp.dot(a, b, preferred_element_type=F32, precision=lax.Precision.HIGHEST)


def edges_kernel(occ, draws, low, high, obuf, dbuf, sems):
    reals, height, width = occ.shape
    copies = []
    for side, start in ((0, 0), (1, height - 8)):
        copies.append(
            pltpu.make_async_copy(occ.at[:, pl.ds(start, 8), :], obuf.at[side], sems.at[side, 0])
        )
        copies.append(
            pltpu.make_async_copy(
                draws.at[pl.ds(0, 3), :, pl.ds(start, 8), :], dbuf.at[side], sems.at[side, 1]
            )
        )
    for copy in copies:
        copy.start()
    even = even_lanes((8, LANES))
    row = iota((8, LANES), 0)
    even_row = row % 2 == 0

    def by_colour(x):
        swapped = jnp.where(even_row, pltpu.roll(x, 7, 0), pltpu.roll(x, 1, 0))
        return jnp.where(even, x, swapped)

    for side, out in ((0, low), (1, high)):
        copies[2 * side].wait()
        copies[2 * side + 1].wait()
        for r in range(reals):
            for c in range(width // LANES):
                lanes = slice(c * LANES, (c + 1) * LANES)
                first = by_colour(obuf[side, r, :, lanes].astype(F32))
                d0, d1, d2 = (
                    by_colour(dbuf[side, w, r, :, lanes].astype(F32)) for w in range(3)
                )
                mixed = pltpu.roll(jnp.where(even_row, d0, d1), 4, 0)
                if side == 0:
                    message = jnp.where(row < 4, first, jnp.where(row == 7, pltpu.roll(d2, 7, 0), mixed))
                else:
                    message = jnp.where(row >= 4, first, jnp.where(row == 1, pltpu.roll(d2, 3, 0), mixed))
                out[r, c] = message.astype(BF16)


def halo_rows(below, above, name):
    row = iota(below.shape, 0)
    moves = {
        "p0": ((2, 1), (0, 7)),
        "p1": ((1, 0), (7, 6)),
        "u0": ((6, 5), (4, 3)),
        "u1": ((4, 4), (3, 3)),
        "u2": ((6, 6), (1, 1)),
    }[name]
    (a6, a7), (b0, b1) = moves

    def moved(x, by):
        return x if by == 0 else pltpu.roll(x, by, 0)

    top = moved(above, a7) if a6 == a7 else jnp.where(row == 6, moved(above, a6), moved(above, a7))
    low = moved(below, b0) if b0 == b1 else jnp.where(row == 0, moved(below, b0), moved(below, b1))
    return top, low


NAMES = ("p0", "p1", "u0", "u1", "u2")


def tile_kernel(occ, draws, frames, strips, part, obuf, dbuf, natural, state, sums, sems):
    reals, height, width = occ.shape
    pairs = height // 2
    tiles = width // LANES
    sweeps = draws.shape[0]

    def copies(r):
        out = [
            pltpu.make_async_copy(
                occ.at[r, :, pl.ds(c * LANES, LANES)], obuf.at[r, c], sems.at[r, c]
            )
            for c in range(tiles)
        ]
        out.append(pltpu.make_async_copy(draws.at[:, r], dbuf.at[r], sems.at[r, tiles]))
        return out

    @pl.loop(0, reals)
    def _(r):
        for copy in copies(r):
            copy.start()

    even = even_lanes((pairs, LANES))
    lane = iota((pairs, LANES), 1)
    sums[...] = jnp.zeros_like(sums)
    strips[...] = jnp.zeros_like(strips)
    for colour in range(2):
        for c in range(tiles):
            state[colour, c, 0:8] = jnp.zeros((8, LANES), F32)
            state[colour, c, pairs + 8 : pairs + 16] = jnp.zeros((8, LANES), F32)

    @pl.loop(0, reals)
    def _(r):
        for copy in copies(r):
            copy.wait()
        group = lane // GROUP == r
        from_left = group & (lane % GROUP >= BLOCK)

        def keep_edges(index, c, value):
            frames[index, r, 0, c] = value[0:8]
            frames[index, r, 1, c] = value[pairs - 8 : pairs]
            if c == 0:
                strips[index, 0] = jnp.where(
                    from_left, pltpu.roll(value, r * GROUP + BLOCK, 1), strips[index, 0]
                )
            if c == tiles - 1:
                strips[index, 1] = jnp.where(
                    group, pltpu.roll(value, r * GROUP + 12, 1), strips[index, 1]
                )

        for c in range(tiles):
            first = obuf[r, c, pl.ds(0, pairs, stride=2)].astype(F32)
            second = obuf[r, c, pl.ds(1, pairs, stride=2)].astype(F32)
            p0 = jnp.where(even, first, second)
            p1 = jnp.where(even, second, first)
            state[0, c, 8 : 8 + pairs] = p0
            state[1, c, 8 : 8 + pairs] = p1
            keep_edges(0, c, p0)
            keep_edges(1, c, p1)
        for w in range(sweeps):
            colour = w % 2
            for c in range(tiles):
                natural[w, c] = dbuf[r, w, :, c * LANES : (c + 1) * LANES].astype(F32)
            for c in range(tiles):
                first = natural[w, c, pl.ds(0, pairs, stride=2)]
                second = natural[w, c, pl.ds(1, pairs, stride=2)]
                draw = jnp.where(even, first, second) if colour == 0 else jnp.where(even, second, first)
                keep_edges(2 + w, c, draw)
                other = 1 - colour
                here = state[other, c, 8 : 8 + pairs]
                up = state[other, c, 7 : 7 + pairs]
                down = state[other, c, 9 : 9 + pairs]
                vertical = jnp.where(even, up, down) if colour == 0 else jnp.where(even, down, up)
                left = state[other, (c - 1) % tiles, 8 : 8 + pairs]
                right = state[other, (c + 1) % tiles, 8 : 8 + pairs]
                left = pltpu.roll(jnp.where(lane == LANES - 1, left, here), 1, 1)
                right = pltpu.roll(jnp.where(lane == 0, right, here), LANES - 1, 1)
                new = updated(
                    state[colour, c, 8 : 8 + pairs], (here + vertical) + (left + right), draw
                )
                state[colour, c, 8 : 8 + pairs] = new
                if w == sweeps - 3 or w == sweeps - 1:
                    snapshot = 0 if w == sweeps - 3 else 1
                    sums[snapshot, c] += here + new

    half = pairs // 2
    total = jnp.zeros((2 * half, LANES), F32)
    for c in range(tiles):
        rows = jnp.concatenate(
            [
                sums[s, c, pl.ds(0, half, stride=2)] + sums[s, c, pl.ds(1, half, stride=2)]
                for s in range(2)
            ]
        )
        total += exact_dot(rows, fold_lanes(LANES, c * (LANES // BLOCK)))
    part[0] = total[:half]
    part[1] = total[half:]


def strips_kernel(below, above, strips, message, corners):
    reals, tiles = below.shape[:2]
    pairs = strips.shape[2]
    lane = iota((8, LANES), 1)
    for v, source in ((0, above), (1, below)):
        sides = [jnp.zeros((8, LANES), F32) for _ in range(2)]
        for r in range(reals):
            group = lane // GROUP == r
            left = pltpu.roll(source[r, 0].astype(F32), r * GROUP + BLOCK, 1)
            right = pltpu.roll(source[r, tiles - 1].astype(F32), (r * GROUP + 12) % LANES, 1)
            sides[0] = jnp.where(group & (lane % GROUP >= BLOCK), left, sides[0])
            sides[1] = jnp.where(group, right, sides[1])
        corners[0, v] = sides[0]
        corners[1, v] = sides[1]
        message[len(NAMES) * pairs + 8 * v : len(NAMES) * pairs + 8 * v + 8] = jnp.where(
            lane % GROUP < 8, sides[0], sides[1]
        ).astype(BF16)
    lane = iota((pairs, LANES), 1)
    for index in range(len(NAMES)):
        message[index * pairs : (index + 1) * pairs] = jnp.where(
            lane % GROUP < 8, strips[index, 0], strips[index, 1]
        ).astype(BF16)


def rows_kernel(below, above, frames, out, arrays):
    reals, tiles = below.shape[:2]
    sweeps = frames.shape[0] - 2
    even = even_lanes((8, LANES))
    lane = iota((8, LANES), 1)
    row = iota((8, LANES), 0)
    sides = range(2)
    for r in range(reals):
        for c in range(tiles):
            low = below[r, c].astype(F32)
            high = above[r, c].astype(F32)
            for index, name in enumerate(NAMES):
                top, bottom = halo_rows(low, high, name)
                arrays[index, r, 0, c] = jnp.where(row >= 6, top, frames[index, r, 0, c])
                arrays[index, r, 1, c] = jnp.where(row < 2, bottom, frames[index, r, 1, c])
    sums = [[[None] * tiles for _ in sides] for _ in range(2)]
    for w in range(sweeps):
        colour = w % 2
        other = 1 - colour
        for r in range(reals):
            for side in sides:
                for c in range(tiles):
                    draw = arrays[2 + w, r, side, c] if w < 3 else frames[2 + w, r, side, c]
                    here = arrays[other, r, side, c]
                    up = pltpu.roll(here, 1, 0)
                    down = pltpu.roll(here, 7, 0)
                    vertical = jnp.where(even, up, down) if colour == 0 else jnp.where(even, down, up)
                    left = arrays[other, r, side, (c - 1) % tiles]
                    right = arrays[other, r, side, (c + 1) % tiles]
                    left = pltpu.roll(jnp.where(lane == LANES - 1, left, here), 1, 1)
                    right = pltpu.roll(jnp.where(lane == 0, right, here), LANES - 1, 1)
                    new = updated(
                        arrays[colour, r, side, c], (here + vertical) + (left + right), draw
                    )
                    arrays[colour, r, side, c] = new
                    if w == sweeps - 3 or w == sweeps - 1:
                        s = 0 if w == sweeps - 3 else 1
                        both = here + new
                        before = sums[s][side][c]
                        sums[s][side][c] = both if before is None else before + both
    total = jnp.zeros((8, LANES), F32)
    for c in range(tiles):
        rows = jnp.zeros((8, LANES), F32)
        for s in range(2):
            for side in sides:
                both = sums[s][side][c]
                both = both + pltpu.roll(both, 1, 0)
                index = 2 * s + side
                shift = (index - (1 if side == 0 else 7)) % 8
                both = both if shift == 0 else pltpu.roll(both, shift, 0)
                rows = jnp.where(row == index, both, rows)
        total += exact_dot(rows, fold_lanes(LANES, c * (LANES // BLOCK)))
    out[...] = total


def columns_kernel(strips, corners, from_left, from_right, part, rows, out, arrays):
    pairs = strips.shape[2]
    sweeps = strips.shape[0] - 2
    base = 16
    count = len(NAMES)
    lane = iota((pairs, LANES), 1) % GROUP
    lane8 = iota((8, LANES), 1) % GROUP
    row8 = iota((8, LANES), 0)

    def joined(side, q, own, left, right):
        if side == 0:
            return jnp.where(q < BLOCK, pltpu.roll(left, LANES - 8, 1), own)
        return jnp.where(q >= GROUP - BLOCK, pltpu.roll(right, 8, 1), own)

    zero = jnp.zeros((8, LANES), F32)
    for side in range(2):
        for index in range(count):
            rows_of = slice(index * pairs, (index + 1) * pairs)
            arrays[index, side, base : base + pairs] = joined(
                side, lane, strips[index, side], from_left[rows_of].astype(F32), from_right[rows_of].astype(F32)
            )
        halos = []
        for v in range(2):
            rows_of = slice(count * pairs + 8 * v, count * pairs + 8 * v + 8)
            halos.append(
                joined(side, lane8, corners[side, v], from_left[rows_of].astype(F32), from_right[rows_of].astype(F32))
            )
        for index, name in enumerate(NAMES):
            top, bottom = halo_rows(halos[1], halos[0], name)
            arrays[index, side, base - 8 : base] = jnp.where(row8 >= 6, top, 0.0)
            arrays[index, side, base + pairs : base + pairs + 8] = jnp.where(row8 < 2, bottom, 0.0)
            if index < 2:
                arrays[index, side, 0 : base - 8] = zero
                arrays[index, side, base + pairs + 8 : base + pairs + 16] = zero
        arrays[count, side, base : base + pairs] = strips[count, side]
        arrays[count, side, base - 8 : base] = zero
        arrays[count, side, base + pairs : base + pairs + 8] = zero
    half = pairs // 2
    sums = [[None, None], [None, None]]
    for w in range(sweeps):
        colour = w % 2
        other = 1 - colour
        grow = 8 if w < sweeps - 1 else 0
        start, size = base - grow, pairs + 2 * grow
        even = even_lanes((size, LANES))
        for side in range(2):
            here = arrays[other, side, start : start + size]
            up = arrays[other, side, start - 1 : start - 1 + size]
            down = arrays[other, side, start + 1 : start + 1 + size]
            vertical = jnp.where(even, up, down) if colour == 0 else jnp.where(even, down, up)
            beside = (here + vertical) + (pltpu.roll(here, 1, 1) + pltpu.roll(here, LANES - 1, 1))
            new = updated(
                arrays[colour, side, start : start + size], beside, arrays[2 + w, side, start : start + size]
            )
            arrays[colour, side, start : start + size] = new
            if w == sweeps - 3 or w == sweeps - 1:
                s = 0 if w == sweeps - 3 else 1
                arrays[count + 1 + s, side, base : base + pairs] = (here + new)[grow : grow + pairs]
    source = iota((LANES, LANES), 0) % GROUP
    target = iota((LANES, LANES), 1)
    total = jnp.zeros((2 * half, LANES), F32)
    for side in range(2):
        rows_of = jnp.concatenate(
            [
                arrays[count + 1 + s, side, pl.ds(base, half, stride=2)]
                + arrays[count + 1 + s, side, pl.ds(base + 1, half, stride=2)]
                for s in range(2)
            ]
        )
        first = BLOCK if side == 0 else 2 * BLOCK
        pick = (source >= first) & (source < first + BLOCK) & (target == (0 if side == 0 else LANES - 1))
        total += exact_dot(rows_of, jnp.where(pick, 1.0, 0.0).astype(F32))
    row = iota((half, LANES), 0)
    column = iota((half, LANES), 1)
    for s in range(2):
        value = part[s]
        value = jnp.where(row == 0, rows[2 * s : 2 * s + 1], value)
        value = jnp.where(row == half - 1, rows[2 * s + 1 : 2 * s + 2], value)
        edge = (column == 0) | (column == LANES - 1)
        out[s] = jnp.where(edge, total[s * half : (s + 1) * half], value)


def shifted(value, axis, by):
    count = lax.axis_size(axis)
    if count == 1:
        return value
    return lax.ppermute(value, axis, [(i, (i + by) % count) for i in range(count)])


def both_ways(to_low, to_high, axis):
    return shifted(to_low, axis, -1), shifted(to_high, axis, 1)


def call(kernel, args, outs, name, vmem, scratch=(), flops=0, space=pltpu.VMEM):
    return pl.pallas_call(
        kernel,
        out_shape=tuple(pltpu.VMEM(shape, dtype) for shape, dtype in outs),
        in_specs=[pl.BlockSpec(memory_space=space) for _ in args],
        out_specs=tuple(pl.BlockSpec(memory_space=pltpu.VMEM) for _ in outs),
        scratch_shapes=list(scratch),
        name=name,
        compiler_params=pltpu.CompilerParams(vmem_limit_bytes=vmem * MIB),
        cost_estimate=pl.CostEstimate(flops=flops, bytes_accessed=0, transcendentals=0),
    )(*args)


def per_device(occupancy, random_draws):
    reals, height, width = occupancy.shape
    sweeps = random_draws.shape[0]
    tiles, pairs, half = width // LANES, height // 2, height // BLOCK
    edge = ((reals, tiles, 8, LANES), BF16)
    low, high = call(
        edges_kernel,
        (occupancy, random_draws),
        (edge, edge),
        "edges",
        8,
        (
            pltpu.VMEM((2, reals, 8, width), jnp.int32),
            pltpu.VMEM((2, 3, reals, 8, width), BF16),
            pltpu.SemaphoreType.DMA((2, 2)),
        ),
        1_000_000,
        pl.ANY,
    )
    below, above = both_ways(low, high, "gx")
    frames, strips, part = call(
        tile_kernel,
        (occupancy, random_draws),
        (
            ((2 + sweeps, reals, 2, tiles, 8, LANES), F32),
            ((2 + sweeps, 2, pairs, LANES), F32),
            ((2, half, LANES), F32),
        ),
        "tile",
        24,
        (
            pltpu.VMEM((reals, tiles, height, LANES), jnp.int32),
            pltpu.VMEM((reals, sweeps, height, width), BF16),
            pltpu.VMEM((sweeps, tiles, height, LANES), F32),
            pltpu.VMEM((2, tiles, pairs + 16, LANES), F32),
            pltpu.VMEM((2, tiles, pairs, LANES), F32),
            pltpu.SemaphoreType.DMA((reals, tiles + 1)),
        ),
        40_000_000,
        pl.ANY,
    )
    message, corners = call(
        strips_kernel,
        (below, above, strips),
        (((len(NAMES) * pairs + 16, LANES), BF16), ((2, 2, 8, LANES), F32)),
        "strips",
        4,
        (),
        1_000_000,
    )
    if lax.axis_size("gy") == 2:
        from_left = from_right = shifted(message, "gy", 1)
    else:
        from_right, from_left = both_ways(message, message, "gy")
    (rows,) = call(
        rows_kernel,
        (below, above, frames),
        (((8, LANES), F32),),
        "rows",
        8,
        (pltpu.VMEM((len(NAMES), reals, 2, tiles, 8, LANES), F32),),
        10_000_000,
    )
    (mine,) = call(
        columns_kernel,
        (strips, corners, from_left, from_right, part, rows),
        (((2, half, LANES), F32),),
        "columns",
        8,
        (pltpu.VMEM((len(NAMES) + 3, 2, pairs + 32, LANES), F32),),
        4_000_000,
    )
    count = lax.axis_size("row")
    if count == 4:
        one, two, three = (shifted(mine, "row", by) for by in (1, 2, 3))
        coarse_sums = (mine + two) + (one + three)
    else:
        coarse_sums = lax.psum(mine, "row")
    averages = coarse_sums * jnp.float32(1.0 / (reals * count * BLOCK * BLOCK))
    coverage = averages[1]
    projected = coverage + LEAP / 2.0 * (coverage - averages[0])
    return (coverage, projected)


def solution(mesh):
    in_specs = (P("row", "gx", "gy"), P(None, "row", "gx", "gy"))
    out_specs = (P("gx", "gy"), P("gx", "gy"))
    return jax.shard_map(
        per_device, mesh=mesh, in_specs=in_specs, out_specs=out_specs, check_vma=False
    )
```

time: 109 us -> 28.6 us (0.26)
  local copies, waits for them, and re-layouts: 43.4 us -> 3.78 us
  other arithmetic: 30.1 us -> 0.63 us
  blocking collectives: 19.3 us -> 0 us
  Pallas kernels: 0 us -> 9.26 us
  starting transfers between devices: 11.8 us -> 8.72 us
  waiting for transfers between devices: 3.33 us -> 5.36 us
    another operation x4 -> x0, local copies, waits for them, and re-layouts: 30.5 us -> none  [per_device(): snapshots = jnp.stack([jnp.sum(earlier, axis=0), jnp.sum(occupied, axis=0)])]
    psum x1 -> x0, blocking collectives: 19.3 us -> none  [per_device(): coarse_sums = lax.psum(block_sums(snapshots), 'row')]
    pallas_call x0 -> x5, Pallas kernels: none -> 9.26 us  [call(): pl.pallas_call(kernel, out_shape=tuple((pltpu.VMEM(shape, dtype) for shap...]
    reduce_sum x3 -> x0, other arithmetic: 9.14 us -> none  [the longest x2 9.11 us: per_device(): snapshots = jnp.stack([jnp.sum(earlier, axis=0), jnp.sum(occupied, axis=0)])]
    select_n x2 -> x0, other arithmetic: 8.46 us -> none  [sublattice_update(): return jnp.where(chosen[None], updated, centre)]
    concatenate x5 -> x0, other arithmetic: 8.14 us -> none  [padded_2(): block = jnp.concatenate([low, block, high], axis=dim)]
    ppermute x6 -> x0, local copies, waits for them, and re-layouts: 4.81 us -> none  [the longest x3 2.76 us: padded_2(): lax.ppermute(lax.slice_in_dim(block, 0, width, axis=dim), axis, backward)]
    slice x12 -> x0, local copies, waits for them, and re-layouts: 4.22 us -> none  [the longest x1 1.51 us: per_device(): random_draws[2 * pair_index + 1].astype(jnp.float32)]
  transfers between devices with their start and end apart: 12 -> 6, of which waited for: 3 -> 4; matrix products, arithmetic and copies ran while one was open for 27% -> 0% of each run, Pallas kernels for 0% -> 29%
where the time goes in v1:
time: 28.6 us; the launch traced here: 28.4 us
  Pallas kernels  9.26 us (32%)
  starting transfers between devices  8.72 us (30%)
  waiting for transfers between devices  5.36 us (19%)
  local copies, waits for them, and re-layouts  3.78 us (13%)
  between operations  0.7 us (2%)
  other arithmetic  0.63 us (2%)
    pallas_call x5, Pallas kernels, call(): pl.pallas_call(kernel, out_shape=tuple((pltpu.VMEM(shape, dtype) for shap...  9.26 us
    ppermute x6, starting transfers between devices, shifted(): lax.ppermute(value, axis, [(i, (i + by) % count) for i in range(count)])  8.72 us
    ppermute x6, waiting for transfers between devices, shifted(): lax.ppermute(value, axis, [(i, (i + by) % count) for i in range(count)])  5.36 us
    unnamed x8, local copies, waits for them, and re-layouts  3.78 us
    add x1, other arithmetic, per_device(): projected = coverage + LEAP / 2.0 * (coverage - averages[0])  0.62 us
  transfers between devices with their start and end apart: 6, of which 4 were waited for; matrix products, arithmetic and copies ran while one was open for 0% of the time, Pallas kernels for 29%

profile of v1, /device:TPU:0, one launch (start us, length us, event | category | flops | bytes accessed | tf_op | source)
XLA Modules:
  0.0 28.4 jit_solution(5847835032041973325)
XLA Ops:
  0.6 0.0 copy-start
  0.6 2.2 %copy-done = bf16[4,8,128,512]{3,2,1,0:T(8,128)(2,1)S(1)} copy-done((bf16[4,8,128,512]{3,2,1,0:T(8,128)(2,1)S(1)}, bf16[4,8,128,512]{3,2,1,0:T(8,128)(2,1)}, u32[]{:S(2)}) %copy-start) | copy-done | bytes 4194328
  2.8 0.0 copy-start.2
  2.8 1.6 %copy-done.2 = s32[8,128,512]{2,1,0:T(8,128)S(1)} copy-done((s32[8,128,512]{2,1,0:T(8,128)S(1)}, s32[8,128,512]{2,1,0:T(8,128)}, u32[]{:S(2)}) %copy-start.2) | copy-done | bytes 2097176
  4.4 0.0 copy-start.1
  4.4 0.0 copy-start.3
  4.4 0.4 %edges.1 = (bf16[8,4,8,128]{3,2,1,0:T(8,128)(2,1)S(1)}, bf16[8,4,8,128]{3,2,1,0:T(8,128)(2,1)S(1)}) custom-call(s32[8,128,512]{2,1,0:T(8,128)S(1)} %copy-done.2, bf16[4,8,128,512]{3,2,1,0:T(8,128)(2,1)S(1)} %copy-done), custom_call_target="tpu_custom_call" | custom-call | flops 1000000 | tf_op jit(solution)/shard_map/edges/pallas_call | solution.py:385
  4.8 4.0 %collective-permute-start = (bf16[8,4,8,128]{3,2,1,0:T(8,128)(2,1)S(1)}, bf16[8,4,8,128]{3,2,1,0:T(8,128)(2,1)S(1)}, u32[]{:S(2)}, u32[]{:S(2)}) collective-permute-start(bf16[8,4,8,128]{3,2,1,0:T(8,128)(2,1)S(1)} %get-tuple-element.10), channel_id=1, source_target_pairs={{0,24},{8,0},{16,8},{24,16},{1,25},{9,1},{17,9},{25,17},{2,26},{10... | collective-permute-start | bytes 196616 | tf_op jit(solution)/shard_map/ppermute | solution.py:377
  8.8 0.0 collective-permute-start.1
  8.8 0.0 copy-done.1
  8.8 0.0 copy-done.3
  8.8 7.0 %tile.1 = (f32[6,8,2,4,8,128]{5,4,3,2,1,0:T(8,128)S(1)}, f32[6,2,64,128]{3,2,1,0:T(8,128)S(1)}, f32[2,32,128]{2,1,0:T(8,128)S(1)}) custom-call(s32[8,128,512]{2,1,0:T(8,128)S(1)} %copy-done.3, bf16[4,8,128,512]{3,2,1,0:T(8,128)(2,1)S(1)} %copy-done.1), custom_call_target="tpu_custom_call" | custom-call | flops 40000000 | tf_op jit(solution)/shard_map/tile/pallas_call | solution.py:385
  15.8 0.0 collective-permute-done.below
  15.8 0.0 collective-permute-done.1.above
  15.8 0.1 strips.1
  15.9 0.1 collective-permute-start.2
  16.0 1.1 %rows.1 = f32[8,128]{1,0:T(8,128)S(1)} custom-call(bf16[8,4,8,128]{3,2,1,0:T(8,128)(2,1)S(1)} %collective-permute-done.below, bf16[8,4,8,128]{3,2,1,0:T(8,128)(2,1)S(1)} %collective-permute-done.1.above, f32[6,8,2,4,8,128]{5,4,3,2,1,0:T(8,128)S(1)} %get-tuple-element.15.frames), custom_call_target="tpu_custom_call" | custom-call | flops 10000000 | tf_op jit(solution)/shard_map/rows/pallas_call | solution.py:385
  17.1 0.2 collective-permute-done.2.from_left.from_right
  17.3 0.7 %columns.1 = f32[2,32,128]{2,1,0:T(8,128)S(1)} custom-call(f32[6,2,64,128]{3,2,1,0:T(8,128)S(1)} %get-tuple-element.9.strips, f32[2,2,8,128]{3,2,1,0:T(8,128)S(1)} %get-tuple-element.12.corners, bf16[336,128]{1,0:T(8,128)(2,1)S(1)} %collective-permute-done.2.from_left.from_right, bf16[336,128]{1,0:T(8,128)(2,1)S(1)} %collective-permute-done.2.from_left.from_right, ...), custom_call_target="tpu_custom_call" | custom-call | flops 4000000 | tf_op jit(solution)/shard_map/columns/pallas_call | solution.py:385
  17.9 3.7 %collective-permute-start.5 = (f32[2,32,128]{2,1,0:T(8,128)S(1)}, f32[2,32,128]{2,1,0:T(8,128)S(1)}, u32[]{:S(2)}, u32[]{:S(2)}) collective-permute-start(f32[2,32,128]{2,1,0:T(8,128)S(1)} %columns.1), channel_id=1, source_target_pairs={{0,3},{1,0},{2,1},{3,2},{4,7},{5,4},{6,5},{7,6},{8,11},{9,8},{10,9... | collective-permute-start | bytes 98312 | tf_op jit(solution)/shard_map/ppermute | solution.py:377
  21.6 0.0 collective-permute-start.4
  21.6 1.0 %collective-permute-start.3 = (f32[2,32,128]{2,1,0:T(8,128)S(1)}, f32[2,32,128]{2,1,0:T(8,128)S(1)}, u32[]{:S(2)}, u32[]{:S(2)}) collective-permute-start(f32[2,32,128]{2,1,0:T(8,128)S(1)} %columns.1), channel_id=1, source_target_pairs={{0,2},{1,3},{2,0},{3,1},{4,6},{5,7},{6,4},{7,5},{8,10},{9,11},{10,... | collective-permute-start | bytes 98312 | tf_op jit(solution)/shard_map/ppermute | solution.py:377
  22.6 0.8 %collective-permute-done.5 = f32[2,32,128]{2,1,0:T(8,128)S(1)} collective-permute-done((f32[2,32,128]{2,1,0:T(8,128)S(1)}, f32[2,32,128]{2,1,0:T(8,128)S(1)}, u32[]{:S(2)}, u32[]{:S(2)}) %collective-permute-start.5) | collective-permute-done | bytes 32800 | tf_op jit(solution)/shard_map/ppermute | solution.py:377
  23.4 3.9 %collective-permute-done.4 = f32[2,32,128]{2,1,0:T(8,128)S(1)} collective-permute-done((f32[2,32,128]{2,1,0:T(8,128)S(1)}, f32[2,32,128]{2,1,0:T(8,128)S(1)}, u32[]{:S(2)}, u32[]{:S(2)}) %collective-permute-start.4) | collective-permute-done | bytes 32800 | tf_op jit(solution)/shard_map/ppermute | solution.py:377
  27.3 0.5 %collective-permute-done.3 = f32[2,32,128]{2,1,0:T(8,128)S(1)} collective-permute-done((f32[2,32,128]{2,1,0:T(8,128)S(1)}, f32[2,32,128]{2,1,0:T(8,128)S(1)}, u32[]{:S(2)}, u32[]{:S(2)}) %collective-permute-start.3) | collective-permute-done | bytes 32800 | tf_op jit(solution)/shard_map/ppermute | solution.py:377
  27.8 0.6 %fusion.2 = (f32[32,128]{1,0:T(8,128)}, f32[32,128]{1,0:T(8,128)}) fusion(f32[2,32,128]{2,1,0:T(8,128)S(1)} %add_multiply_fusion), kind=kLoop, calls=%fused_computation.4 | loop fusion | flops 12288 | bytes 65536 | tf_op jit(solution)/shard_map/add | solution.py:477
  (1 shorter events, 0.0 us)
Async XLA Ops:
  0.6 2.2 %copy-start = (bf16[4,8,128,512]{3,2,1,0:T(8,128)(2,1)S(1)}, bf16[4,8,128,512]{3,2,1,0:T(8,128)(2,1)}, u32[]{:S(2)}) copy-start(bf16[4,8,128,512]{3,2,1,0:T(8,128)(2,1)} %draws.3) | copy-start | bytes 12582916
  2.8 1.6 %copy-start.2 = (s32[8,128,512]{2,1,0:T(8,128)S(1)}, s32[8,128,512]{2,1,0:T(8,128)}, u32[]{:S(2)}) copy-start(s32[8,128,512]{2,1,0:T(8,128)} %occ.3) | copy-start | bytes 6291460
  4.4 4.4 %copy-start.1 = (bf16[4,8,128,512]{3,2,1,0:T(8,128)(2,1)S(1)}, bf16[4,8,128,512]{3,2,1,0:T(8,128)(2,1)}, u32[]{:S(2)}) copy-start(bf16[4,8,128,512]{3,2,1,0:T(8,128)(2,1)} %draws.3) | copy-start | bytes 12582916
  4.4 4.4 %copy-start.3 = (s32[8,128,512]{2,1,0:T(8,128)S(1)}, s32[8,128,512]{2,1,0:T(8,128)}, u32[]{:S(2)}) copy-start(s32[8,128,512]{2,1,0:T(8,128)} %occ.3) | copy-start | bytes 6291460
  4.8 11.0 %collective-permute-start = (bf16[8,4,8,128]{3,2,1,0:T(8,128)(2,1)S(1)}, bf16[8,4,8,128]{3,2,1,0:T(8,128)(2,1)S(1)}, u32[]{:S(2)}, u32[]{:S(2)}) collective-permute-start(bf16[8,4,8,128]{3,2,1,0:T(8,128)(2,1)S(1)} %get-tuple-element.10), channel_id=1, source_target_pairs={{0,24},{8,0},{16,8},{24,16},{1,25},{9,1},{17,9},{25,17},{2,26},{10... | collective-permute-start | bytes 196616 | tf_op jit(solution)/shard_map/ppermute | solution.py:377
  8.8 7.1 %collective-permute-start.1 = (bf16[8,4,8,128]{3,2,1,0:T(8,128)(2,1)S(1)}, bf16[8,4,8,128]{3,2,1,0:T(8,128)(2,1)S(1)}, u32[]{:S(2)}, u32[]{:S(2)}) collective-permute-start(bf16[8,4,8,128]{3,2,1,0:T(8,128)(2,1)S(1)} %get-tuple-element.11), channel_id=1, source_target_pairs={{0,8},{8,16},{16,24},{24,0},{1,9},{9,17},{17,25},{25,1},{2,10},{10... | collective-permute-start | bytes 196616 | tf_op jit(solution)/shard_map/ppermute | solution.py:377
  15.9 1.3 %collective-permute-start.2 = (bf16[336,128]{1,0:T(8,128)(2,1)S(1)}, bf16[336,128]{1,0:T(8,128)(2,1)S(1)}, u32[]{:S(2)}, u32[]{:S(2)}) collective-permute-start(bf16[336,128]{1,0:T(8,128)(2,1)S(1)} %get-tuple-element.13), channel_id=1, source_target_pairs={{0,4},{4,0},{1,5},{5,1},{2,6},{6,2},{3,7},{7,3},{8,12},{12,8},{9,1... | collective-permute-start | bytes 258056 | tf_op jit(solution)/shard_map/ppermute | solution.py:377
  17.9 5.4 %collective-permute-start.5 = (f32[2,32,128]{2,1,0:T(8,128)S(1)}, f32[2,32,128]{2,1,0:T(8,128)S(1)}, u32[]{:S(2)}, u32[]{:S(2)}) collective-permute-start(f32[2,32,128]{2,1,0:T(8,128)S(1)} %columns.1), channel_id=1, source_target_pairs={{0,3},{1,0},{2,1},{3,2},{4,7},{5,4},{6,5},{7,6},{8,11},{9,8},{10,9... | collective-permute-start | bytes 98312 | tf_op jit(solution)/shard_map/ppermute | solution.py:377
  21.6 5.7 %collective-permute-start.4 = (f32[2,32,128]{2,1,0:T(8,128)S(1)}, f32[2,32,128]{2,1,0:T(8,128)S(1)}, u32[]{:S(2)}, u32[]{:S(2)}) collective-permute-start(f32[2,32,128]{2,1,0:T(8,128)S(1)} %columns.1), channel_id=1, source_target_pairs={{0,1},{1,2},{2,3},{3,0},{4,5},{5,6},{6,7},{7,4},{8,9},{9,10},{10,1... | collective-permute-start | bytes 98312 | tf_op jit(solution)/shard_map/ppermute | solution.py:377
  21.6 6.2 %collective-permute-start.3 = (f32[2,32,128]{2,1,0:T(8,128)S(1)}, f32[2,32,128]{2,1,0:T(8,128)S(1)}, u32[]{:S(2)}, u32[]{:S(2)}) collective-permute-start(f32[2,32,128]{2,1,0:T(8,128)S(1)} %columns.1), channel_id=1, source_target_pairs={{0,2},{1,3},{2,0},{3,1},{4,6},{5,7},{6,4},{7,5},{8,10},{9,11},{10,... | collective-permute-start | bytes 98312 | tf_op jit(solution)/shard_map/ppermute | solution.py:377

commit v2 on v1

--- a/solution.py
+++ b/solution.py
@@ -18,6 +18,7 @@
 COUPLING = 0.5
 
 LANES = 128
+CHUNK = 8
 GROUP = 16
 F32 = jnp.float32
 BF16 = jnp.bfloat16
@@ -39,14 +40,28 @@
     return centre * keep + (gain + (0.25 * HOPPING) * beside)
 
 
-def fold_lanes(width, first, rows_per=1):
-    source = iota((width, LANES), 0)
-    target = iota((width, LANES), 1)
-    return jnp.where(source // BLOCK + first == target, 1.0, 0.0).astype(F32)
-
-
-def exact_dot(a, b):
-    return jnp.dot(a, b, preferred_element_type=F32, precision=lax.Precision.HIGHEST)
+def fold_lanes(first):
+    source = iota((LANES, LANES), 0)
+    target = iota((LANES, LANES), 1)
+    return selection(source // BLOCK + first == target)
+
+
+def selection(picked):
+    return jnp.where(picked, 1.0, 0.0).astype(BF16)
+
+
+def split(x):
+    high = x.astype(BF16)
+    rest = x - high.astype(F32)
+    middle = rest.astype(BF16)
+    low = (rest - middle.astype(F32)).astype(BF16)
+    return jnp.concatenate([high, middle, low])
+
+
+def selected(x, matrix):
+    size = x.shape[0]
+    y = jnp.dot(split(x), matrix, preferred_element_type=F32)
+    return (y[:size] + y[size : 2 * size]) + y[2 * size :]
 
 
 def edges_kernel(occ, draws, low, high, obuf, dbuf, sems):
@@ -132,8 +147,8 @@
         for copy in copies(r):
             copy.start()
 
-    even = even_lanes((pairs, LANES))
-    lane = iota((pairs, LANES), 1)
+    even = even_lanes((CHUNK, LANES))
+    lane = iota((CHUNK, LANES), 1)
     sums[...] = jnp.zeros_like(sums)
     strips[...] = jnp.zeros_like(strips)
     for colour in range(2):
@@ -148,52 +163,53 @@
         group = lane // GROUP == r
         from_left = group & (lane % GROUP >= BLOCK)
 
-        def keep_edges(index, c, value):
-            frames[index, r, 0, c] = value[0:8]
-            frames[index, r, 1, c] = value[pairs - 8 : pairs]
+        def keep_edges(index, c, value, start):
+            if start == 0:
+                frames[index, r, 0, c] = value[:8]
+            if start == pairs - CHUNK:
+                frames[index, r, 1, c] = value[CHUNK - 8 :]
+            rows = slice(start, start + CHUNK)
             if c == 0:
-                strips[index, 0] = jnp.where(
-                    from_left, pltpu.roll(value, r * GROUP + BLOCK, 1), strips[index, 0]
-                )
+                pltpu.store(strips.at[index, 0, rows], pltpu.roll(value, r * GROUP + BLOCK, 1), mask=from_left)
             if c == tiles - 1:
-                strips[index, 1] = jnp.where(
-                    group, pltpu.roll(value, r * GROUP + 12, 1), strips[index, 1]
-                )
-
-        for c in range(tiles):
-            first = obuf[r, c, pl.ds(0, pairs, stride=2)].astype(F32)
-            second = obuf[r, c, pl.ds(1, pairs, stride=2)].astype(F32)
-            p0 = jnp.where(even, first, second)
-            p1 = jnp.where(even, second, first)
-            state[0, c, 8 : 8 + pairs] = p0
-            state[1, c, 8 : 8 + pairs] = p1
-            keep_edges(0, c, p0)
-            keep_edges(1, c, p1)
+                pltpu.store(strips.at[index, 1, rows], pltpu.roll(value, r * GROUP + 12, 1), mask=group)
+
+        for start in range(0, pairs, CHUNK):
+            for c in range(tiles):
+                first = obuf[r, c, pl.ds(2 * start, CHUNK, stride=2)].astype(F32)
+                second = obuf[r, c, pl.ds(2 * start + 1, CHUNK, stride=2)].astype(F32)
+                p0 = jnp.where(even, first, second)
+                p1 = jnp.where(even, second, first)
+                state[0, c, 8 + start : 8 + start + CHUNK] = p0
+                state[1, c, 8 + start : 8 + start + CHUNK] = p1
+                keep_edges(0, c, p0, start)
+                keep_edges(1, c, p1, start)
         for w in range(sweeps):
             colour = w % 2
+            other = 1 - colour
             for c in range(tiles):
                 natural[w, c] = dbuf[r, w, :, c * LANES : (c + 1) * LANES].astype(F32)
-            for c in range(tiles):
-                first = natural[w, c, pl.ds(0, pairs, stride=2)]
-                second = natural[w, c, pl.ds(1, pairs, stride=2)]
-                draw = jnp.where(even, first, second) if colour == 0 else jnp.where(even, second, first)
-                keep_edges(2 + w, c, draw)
-                other = 1 - colour
-                here = state[other, c, 8 : 8 + pairs]
-                up = state[other, c, 7 : 7 + pairs]
-                down = state[other, c, 9 : 9 + pairs]
-                vertical = jnp.where(even, up, down) if colour == 0 else jnp.where(even, down, up)
-                left = state[other, (c - 1) % tiles, 8 : 8 + pairs]
-                right = state[other, (c + 1) % tiles, 8 : 8 + pairs]
-                left = pltpu.roll(jnp.where(lane == LANES - 1, left, here), 1, 1)
-                right = pltpu.roll(jnp.where(lane == 0, right, here), LANES - 1, 1)
-                new = updated(
-                    state[colour, c, 8 : 8 + pairs], (here + vertical) + (left + right), draw
-                )
-                state[colour, c, 8 : 8 + pairs] = new
-                if w == sweeps - 3 or w == sweeps - 1:
-                    snapshot = 0 if w == sweeps - 3 else 1
-                    sums[snapshot, c] += here + new
+            for start in range(0, pairs, CHUNK):
+                heres = [state[other, c, 8 + start : 8 + start + CHUNK] for c in range(tiles)]
+                for c in range(tiles):
+                    first = natural[w, c, pl.ds(2 * start, CHUNK, stride=2)]
+                    second = natural[w, c, pl.ds(2 * start + 1, CHUNK, stride=2)]
+                    draw = jnp.where(even, first, second) if colour == 0 else jnp.where(even, second, first)
+                    keep_edges(2 + w, c, draw, start)
+                    here = heres[c]
+                    up = state[other, c, 7 + start : 7 + start + CHUNK]
+                    down = state[other, c, 9 + start : 9 + start + CHUNK]
+                    vertical = jnp.where(even, up, down) if colour == 0 else jnp.where(even, down, up)
+                    left = jnp.where(lane == LANES - 1, heres[(c - 1) % tiles], here)
+                    right = jnp.where(lane == 0, heres[(c + 1) % tiles], here)
+                    beside = pltpu.roll(left, 1, 1) + pltpu.roll(right, LANES - 1, 1)
+                    new = updated(
+                        state[colour, c, 8 + start : 8 + start + CHUNK], (here + vertical) + beside, draw
+                    )
+                    state[colour, c, 8 + start : 8 + start + CHUNK] = new
+                    if w == sweeps - 3 or w == sweeps - 1:
+                        snapshot = 0 if w == sweeps - 3 else 1
+                        sums[snapshot, c, start : start + CHUNK] += here + new
 
     half = pairs // 2
     total = jnp.zeros((2 * half, LANES), F32)
@@ -204,7 +220,7 @@
                 for s in range(2)
             ]
         )
-        total += exact_dot(rows, fold_lanes(LANES, c * (LANES // BLOCK)))
+        total += selected(rows, fold_lanes(c * (LANES // BLOCK)))
     part[0] = total[:half]
     part[1] = total[half:]
 
@@ -284,7 +300,7 @@
                 shift = (index - (1 if side == 0 else 7)) % 8
                 both = both if shift == 0 else pltpu.roll(both, shift, 0)
                 rows = jnp.where(row == index, both, rows)
-        total += exact_dot(rows, fold_lanes(LANES, c * (LANES // BLOCK)))
+        total += selected(rows, fold_lanes(c * (LANES // BLOCK)))
     out[...] = total
 
 
@@ -359,7 +375,7 @@
         )
         first = BLOCK if side == 0 else 2 * BLOCK
         pick = (source >= first) & (source < first + BLOCK) & (target == (0 if side == 0 else LANES - 1))
-        total += exact_dot(rows_of, jnp.where(pick, 1.0, 0.0).astype(F32))
+        total += selected(rows_of, selection(pick))
     row = iota((half, LANES), 0)
     column = iota((half, LANES), 1)
     for s in range(2):
@@ -382,6 +398,8 @@
 
 
 def call(kernel, args, outs, name, vmem, scratch=(), flops=0, space=pltpu.VMEM):
+    if space == pltpu.HBM:
+        args = [pltpu.with_memory_space_constraint(arg, space) for arg in args]
     return pl.pallas_call(
         kernel,
         out_shape=tuple(pltpu.VMEM(shape, dtype) for shape, dtype in outs),
@@ -411,7 +429,7 @@
             pltpu.SemaphoreType.DMA((2, 2)),
         ),
         1_000_000,
-        pl.ANY,
+        pltpu.HBM,
     )
     below, above = both_ways(low, high, "gx")
     frames, strips, part = call(
@@ -433,7 +451,7 @@
             pltpu.SemaphoreType.DMA((reals, tiles + 1)),
         ),
         40_000_000,
-        pl.ANY,
+        pltpu.HBM,
     )
     message, corners = call(
         strips_kernel,
@@ -468,7 +486,7 @@
     )
     count = lax.axis_size("row")
     if count == 4:
-        one, two, three = (shifted(mine, "row", by) for by in (1, 2, 3))
+        one, three, two = (shifted(mine, "row", by) for by in (1, 3, 2))
         coarse_sums = (mine + two) + (one + three)
     else:
         coarse_sums = lax.psum(mine, "row")

time: 28.6 us -> 24.4 us (0.85)
  local copies, waits for them, and re-layouts: 3.78 us -> 0 us
  Pallas kernels: 9.26 us -> 8.86 us
    unnamed x8 -> x0, local copies, waits for them, and re-layouts: 3.78 us -> none
    pallas_call x5, Pallas kernels: 9.26 us -> 8.86 us  [call(): pl.pallas_call(kernel, out_shape=tuple((pltpu.VMEM(shape, dtype) for shap...]
  transfers between devices with their start and end apart: 6 -> 6, of which waited for: 4 -> 4; matrix products, arithmetic and copies ran while one was open for 0% -> 0% of each run, Pallas kernels for 29% -> 28%
where the time goes in v2:
time: 24.4 us; the launch traced here: 24.3 us
  Pallas kernels  8.86 us (36%)
  starting transfers between devices  8.72 us (36%)
  waiting for transfers between devices  5.37 us (22%)
  between operations  0.68 us (3%)
  other arithmetic  0.63 us (3%)
    pallas_call x5, Pallas kernels, call(): pl.pallas_call(kernel, out_shape=tuple((pltpu.VMEM(shape, dtype) for shap...  8.86 us
    ppermute x6, starting transfers between devices, shifted(): lax.ppermute(value, axis, [(i, (i + by) % count) for i in range(count)])  8.72 us
    ppermute x6, waiting for transfers between devices, shifted(): lax.ppermute(value, axis, [(i, (i + by) % count) for i in range(count)])  5.37 us
    add x1, other arithmetic, per_device(): projected = coverage + LEAP / 2.0 * (coverage - averages[0])  0.62 us
  transfers between devices with their start and end apart: 6, of which 4 were waited for; matrix products, arithmetic and copies ran while one was open for 0% of the time, Pallas kernels for 28%

profile of v2, /device:TPU:0, one launch (start us, length us, event | category | flops | bytes accessed | tf_op | source)
XLA Modules:
  0.0 24.3 jit_solution(10366381753386680399)
XLA Ops:
  0.6 1.3 %edges.1 = (bf16[8,4,8,128]{3,2,1,0:T(8,128)(2,1)S(1)}, bf16[8,4,8,128]{3,2,1,0:T(8,128)(2,1)S(1)}) custom-call(s32[8,128,512]{2,1,0:T(8,128)} %occ.3, bf16[4,8,128,512]{3,2,1,0:T(8,128)(2,1)} %draws.3), custom_call_target="tpu_custom_call" | custom-call | flops 1000000 | tf_op jit(solution)/shard_map/edges/pallas_call | solution.py:403
  1.9 4.0 %collective-permute-start = (bf16[8,4,8,128]{3,2,1,0:T(8,128)(2,1)S(1)}, bf16[8,4,8,128]{3,2,1,0:T(8,128)(2,1)S(1)}, u32[]{:S(2)}, u32[]{:S(2)}) collective-permute-start(bf16[8,4,8,128]{3,2,1,0:T(8,128)(2,1)S(1)} %get-tuple-element.10), channel_id=1, source_target_pairs={{0,24},{8,0},{16,8},{24,16},{1,25},{9,1},{17,9},{25,17},{2,26},{10... | collective-permute-start | bytes 196616 | tf_op jit(solution)/shard_map/ppermute | solution.py:393
  5.9 0.0 collective-permute-start.1
  5.9 5.9 %tile.1 = (f32[6,8,2,4,8,128]{5,4,3,2,1,0:T(8,128)S(1)}, f32[6,2,64,128]{3,2,1,0:T(8,128)S(1)}, f32[2,32,128]{2,1,0:T(8,128)S(1)}) custom-call(s32[8,128,512]{2,1,0:T(8,128)} %occ.3, bf16[4,8,128,512]{3,2,1,0:T(8,128)(2,1)} %draws.3), custom_call_target="tpu_custom_call" | custom-call | flops 40000000 | tf_op jit(solution)/shard_map/tile/pallas_call | solution.py:403
  11.8 0.0 collective-permute-done.below
  11.8 0.0 collective-permute-done.1.above
  11.8 0.1 strips.1
  11.9 0.1 collective-permute-start.2
  12.0 1.0 %rows.1 = f32[8,128]{1,0:T(8,128)S(1)} custom-call(bf16[8,4,8,128]{3,2,1,0:T(8,128)(2,1)S(1)} %collective-permute-done.below, bf16[8,4,8,128]{3,2,1,0:T(8,128)(2,1)S(1)} %collective-permute-done.1.above, f32[6,8,2,4,8,128]{5,4,3,2,1,0:T(8,128)S(1)} %get-tuple-element.15.frames), custom_call_target="tpu_custom_call" | custom-call | flops 10000000 | tf_op jit(solution)/shard_map/rows/pallas_call | solution.py:403
  13.0 0.3 %collective-permute-done.2.from_left.from_right = bf16[336,128]{1,0:T(8,128)(2,1)S(1)} collective-permute-done((bf16[336,128]{1,0:T(8,128)(2,1)S(1)}, bf16[336,128]{1,0:T(8,128)(2,1)S(1)}, u32[]{:S(2)}, u32[]{:S(2)}) %collective-permute-start.2) | collective-permute-done | bytes 86048 | tf_op jit(solution)/shard_map/ppermute | solution.py:393
  13.3 0.6 %columns.1 = f32[2,32,128]{2,1,0:T(8,128)S(1)} custom-call(f32[6,2,64,128]{3,2,1,0:T(8,128)S(1)} %get-tuple-element.9.strips, f32[2,2,8,128]{3,2,1,0:T(8,128)S(1)} %get-tuple-element.12.corners, bf16[336,128]{1,0:T(8,128)(2,1)S(1)} %collective-permute-done.2.from_left.from_right, bf16[336,128]{1,0:T(8,128)(2,1)S(1)} %collective-permute-done.2.from_left.from_right, ...), custom_call_target="tpu_custom_call" | custom-call | flops 4000000 | tf_op jit(solution)/shard_map/columns/pallas_call | solution.py:403
  13.9 3.7 %collective-permute-start.5 = (f32[2,32,128]{2,1,0:T(8,128)S(1)}, f32[2,32,128]{2,1,0:T(8,128)S(1)}, u32[]{:S(2)}, u32[]{:S(2)}) collective-permute-start(f32[2,32,128]{2,1,0:T(8,128)S(1)} %columns.1), channel_id=1, source_target_pairs={{0,3},{1,0},{2,1},{3,2},{4,7},{5,4},{6,5},{7,6},{8,11},{9,8},{10,9... | collective-permute-start | bytes 98312 | tf_op jit(solution)/shard_map/ppermute | solution.py:393
  17.6 0.0 collective-permute-start.4
  17.6 1.0 %collective-permute-start.3 = (f32[2,32,128]{2,1,0:T(8,128)S(1)}, f32[2,32,128]{2,1,0:T(8,128)S(1)}, u32[]{:S(2)}, u32[]{:S(2)}) collective-permute-start(f32[2,32,128]{2,1,0:T(8,128)S(1)} %columns.1), channel_id=1, source_target_pairs={{0,2},{1,3},{2,0},{3,1},{4,6},{5,7},{6,4},{7,5},{8,10},{9,11},{10,... | collective-permute-start | bytes 98312 | tf_op jit(solution)/shard_map/ppermute | solution.py:393
  18.6 0.8 %collective-permute-done.5 = f32[2,32,128]{2,1,0:T(8,128)S(1)} collective-permute-done((f32[2,32,128]{2,1,0:T(8,128)S(1)}, f32[2,32,128]{2,1,0:T(8,128)S(1)}, u32[]{:S(2)}, u32[]{:S(2)}) %collective-permute-start.5) | collective-permute-done | bytes 32800 | tf_op jit(solution)/shard_map/ppermute | solution.py:393
  19.3 4.0 %collective-permute-done.4 = f32[2,32,128]{2,1,0:T(8,128)S(1)} collective-permute-done((f32[2,32,128]{2,1,0:T(8,128)S(1)}, f32[2,32,128]{2,1,0:T(8,128)S(1)}, u32[]{:S(2)}, u32[]{:S(2)}) %collective-permute-start.4) | collective-permute-done | bytes 32800 | tf_op jit(solution)/shard_map/ppermute | solution.py:393
  23.3 0.4 %collective-permute-done.3 = f32[2,32,128]{2,1,0:T(8,128)S(1)} collective-permute-done((f32[2,32,128]{2,1,0:T(8,128)S(1)}, f32[2,32,128]{2,1,0:T(8,128)S(1)}, u32[]{:S(2)}, u32[]{:S(2)}) %collective-permute-start.3) | collective-permute-done | bytes 32800 | tf_op jit(solution)/shard_map/ppermute | solution.py:393
  23.6 0.6 %fusion.2 = (f32[32,128]{1,0:T(8,128)}, f32[32,128]{1,0:T(8,128)}) fusion(f32[2,32,128]{2,1,0:T(8,128)S(1)} %add_multiply_fusion), kind=kLoop, calls=%fused_computation.4 | loop fusion | flops 12288 | bytes 65536 | tf_op jit(solution)/shard_map/add | solution.py:495
  (1 shorter events, 0.0 us)
Async XLA Ops:
  1.9 9.9 %collective-permute-start = (bf16[8,4,8,128]{3,2,1,0:T(8,128)(2,1)S(1)}, bf16[8,4,8,128]{3,2,1,0:T(8,128)(2,1)S(1)}, u32[]{:S(2)}, u32[]{:S(2)}) collective-permute-start(bf16[8,4,8,128]{3,2,1,0:T(8,128)(2,1)S(1)} %get-tuple-element.10), channel_id=1, source_target_pairs={{0,24},{8,0},{16,8},{24,16},{1,25},{9,1},{17,9},{25,17},{2,26},{10... | collective-permute-start | bytes 196616 | tf_op jit(solution)/shard_map/ppermute | solution.py:393
  5.9 5.9 %collective-permute-start.1 = (bf16[8,4,8,128]{3,2,1,0:T(8,128)(2,1)S(1)}, bf16[8,4,8,128]{3,2,1,0:T(8,128)(2,1)S(1)}, u32[]{:S(2)}, u32[]{:S(2)}) collective-permute-start(bf16[8,4,8,128]{3,2,1,0:T(8,128)(2,1)S(1)} %get-tuple-element.11), channel_id=1, source_target_pairs={{0,8},{8,16},{16,24},{24,0},{1,9},{9,17},{17,25},{25,1},{2,10},{10... | collective-permute-start | bytes 196616 | tf_op jit(solution)/shard_map/ppermute | solution.py:393
  11.9 1.3 %collective-permute-start.2 = (bf16[336,128]{1,0:T(8,128)(2,1)S(1)}, bf16[336,128]{1,0:T(8,128)(2,1)S(1)}, u32[]{:S(2)}, u32[]{:S(2)}) collective-permute-start(bf16[336,128]{1,0:T(8,128)(2,1)S(1)} %get-tuple-element.13), channel_id=1, source_target_pairs={{0,4},{4,0},{1,5},{5,1},{2,6},{6,2},{3,7},{7,3},{8,12},{12,8},{9,1... | collective-permute-start | bytes 258056 | tf_op jit(solution)/shard_map/ppermute | solution.py:393
  13.9 5.4 %collective-permute-start.5 = (f32[2,32,128]{2,1,0:T(8,128)S(1)}, f32[2,32,128]{2,1,0:T(8,128)S(1)}, u32[]{:S(2)}, u32[]{:S(2)}) collective-permute-start(f32[2,32,128]{2,1,0:T(8,128)S(1)} %columns.1), channel_id=1, source_target_pairs={{0,3},{1,0},{2,1},{3,2},{4,7},{5,4},{6,5},{7,6},{8,11},{9,8},{10,9... | collective-permute-start | bytes 98312 | tf_op jit(solution)/shard_map/ppermute | solution.py:393
  17.6 5.7 %collective-permute-start.4 = (f32[2,32,128]{2,1,0:T(8,128)S(1)}, f32[2,32,128]{2,1,0:T(8,128)S(1)}, u32[]{:S(2)}, u32[]{:S(2)}) collective-permute-start(f32[2,32,128]{2,1,0:T(8,128)S(1)} %columns.1), channel_id=1, source_target_pairs={{0,1},{1,2},{2,3},{3,0},{4,5},{5,6},{6,7},{7,4},{8,9},{9,10},{10,1... | collective-permute-start | bytes 98312 | tf_op jit(solution)/shard_map/ppermute | solution.py:393
  17.6 6.1 %collective-permute-start.3 = (f32[2,32,128]{2,1,0:T(8,128)S(1)}, f32[2,32,128]{2,1,0:T(8,128)S(1)}, u32[]{:S(2)}, u32[]{:S(2)}) collective-permute-start(f32[2,32,128]{2,1,0:T(8,128)S(1)} %columns.1), channel_id=1, source_target_pairs={{0,2},{1,3},{2,0},{3,1},{4,6},{5,7},{6,4},{7,5},{8,10},{9,11},{10,... | collective-permute-start | bytes 98312 | tf_op jit(solution)/shard_map/ppermute | solution.py:393

commit v3 on v2

--- a/solution.py
+++ b/solution.py
@@ -1,4 +1,3 @@
-import functools
 import math
 
 import jax
@@ -8,12 +7,11 @@
 from jax.experimental.pallas import tpu as pltpu
 from jax.sharding import PartitionSpec as P
 
-SWEEPS = 4
+
 BLOCK = 4
 LEAP = 8
 
 ADSORB = 0.6
-DESORB = 0.6
 HOPPING = 0.3
 COUPLING = 0.5
 
@@ -126,26 +124,11 @@
 NAMES = ("p0", "p1", "u0", "u1", "u2")
 
 
-def tile_kernel(occ, draws, frames, strips, part, obuf, dbuf, natural, state, sums, sems):
+def tile_kernel(occ, draws, frames, strips, part, natural, state, sums):
     reals, height, width = occ.shape
     pairs = height // 2
     tiles = width // LANES
     sweeps = draws.shape[0]
-
-    def copies(r):
-        out = [
-            pltpu.make_async_copy(
-                occ.at[r, :, pl.ds(c * LANES, LANES)], obuf.at[r, c], sems.at[r, c]
-            )
-            for c in range(tiles)
-        ]
-        out.append(pltpu.make_async_copy(draws.at[:, r], dbuf.at[r], sems.at[r, tiles]))
-        return out
-
-    @pl.loop(0, reals)
-    def _(r):
-        for copy in copies(r):
-            copy.start()
 
     even = even_lanes((CHUNK, LANES))
     lane = iota((CHUNK, LANES), 1)
@@ -158,8 +141,6 @@
 
     @pl.loop(0, reals)
     def _(r):
-        for copy in copies(r):
-            copy.wait()
         group = lane // GROUP == r
         from_left = group & (lane % GROUP >= BLOCK)
 
@@ -174,10 +155,12 @@
             if c == tiles - 1:
                 pltpu.store(strips.at[index, 1, rows], pltpu.roll(value, r * GROUP + 12, 1), mask=group)
 
+        for c in range(tiles):
+            natural[sweeps, c] = occ[r, :, c * LANES : (c + 1) * LANES].astype(F32)
         for start in range(0, pairs, CHUNK):
             for c in range(tiles):
-                first = obuf[r, c, pl.ds(2 * start, CHUNK, stride=2)].astype(F32)
-                second = obuf[r, c, pl.ds(2 * start + 1, CHUNK, stride=2)].astype(F32)
+                first = natural[sweeps, c, pl.ds(2 * start, CHUNK, stride=2)]
+                second = natural[sweeps, c, pl.ds(2 * start + 1, CHUNK, stride=2)]
                 p0 = jnp.where(even, first, second)
                 p1 = jnp.where(even, second, first)
                 state[0, c, 8 + start : 8 + start + CHUNK] = p0
@@ -188,7 +171,7 @@
             colour = w % 2
             other = 1 - colour
             for c in range(tiles):
-                natural[w, c] = dbuf[r, w, :, c * LANES : (c + 1) * LANES].astype(F32)
+                natural[w, c] = draws[w, r, :, c * LANES : (c + 1) * LANES].astype(F32)
             for start in range(0, pairs, CHUNK):
                 heres = [state[other, c, 8 + start : 8 + start + CHUNK] for c in range(tiles)]
                 for c in range(tiles):
@@ -342,7 +325,6 @@
         arrays[count, side, base - 8 : base] = zero
         arrays[count, side, base + pairs : base + pairs + 8] = zero
     half = pairs // 2
-    sums = [[None, None], [None, None]]
     for w in range(sweeps):
         colour = w % 2
         other = 1 - colour
@@ -394,10 +376,12 @@
 
 
 def both_ways(to_low, to_high, axis):
-    return shifted(to_low, axis, -1), shifted(to_high, axis, 1)
-
-
-def call(kernel, args, outs, name, vmem, scratch=(), flops=0, space=pltpu.VMEM):
+    before = shifted(to_high, axis, 1)
+    after = shifted(to_low, axis, -1)
+    return after, before
+
+
+def call(kernel, args, outs, vmem, scratch=(), flops=0, space=pltpu.VMEM):
     if space == pltpu.HBM:
         args = [pltpu.with_memory_space_constraint(arg, space) for arg in args]
     return pl.pallas_call(
@@ -406,13 +390,12 @@
         in_specs=[pl.BlockSpec(memory_space=space) for _ in args],
         out_specs=tuple(pl.BlockSpec(memory_space=pltpu.VMEM) for _ in outs),
         scratch_shapes=list(scratch),
-        name=name,
         compiler_params=pltpu.CompilerParams(vmem_limit_bytes=vmem * MIB),
         cost_estimate=pl.CostEstimate(flops=flops, bytes_accessed=0, transcendentals=0),
     )(*args)
 
 
-def per_device(occupancy, random_draws):
+def integrated(occupancy, random_draws):
     reals, height, width = occupancy.shape
     sweeps = random_draws.shape[0]
     tiles, pairs, half = width // LANES, height // 2, height // BLOCK
@@ -421,7 +404,6 @@
         edges_kernel,
         (occupancy, random_draws),
         (edge, edge),
-        "edges",
         8,
         (
             pltpu.VMEM((2, reals, 8, width), jnp.int32),
@@ -440,24 +422,18 @@
             ((2 + sweeps, 2, pairs, LANES), F32),
             ((2, half, LANES), F32),
         ),
-        "tile",
         24,
         (
-            pltpu.VMEM((reals, tiles, height, LANES), jnp.int32),
-            pltpu.VMEM((reals, sweeps, height, width), BF16),
-            pltpu.VMEM((sweeps, tiles, height, LANES), F32),
+            pltpu.VMEM((sweeps + 1, tiles, height, LANES), F32),
             pltpu.VMEM((2, tiles, pairs + 16, LANES), F32),
             pltpu.VMEM((2, tiles, pairs, LANES), F32),
-            pltpu.SemaphoreType.DMA((reals, tiles + 1)),
         ),
         40_000_000,
-        pltpu.HBM,
     )
     message, corners = call(
         strips_kernel,
         (below, above, strips),
         (((len(NAMES) * pairs + 16, LANES), BF16), ((2, 2, 8, LANES), F32)),
-        "strips",
         4,
         (),
         1_000_000,
@@ -470,7 +446,6 @@
         rows_kernel,
         (below, above, frames),
         (((8, LANES), F32),),
-        "rows",
         8,
         (pltpu.VMEM((len(NAMES), reals, 2, tiles, 8, LANES), F32),),
         10_000_000,
@@ -479,15 +454,16 @@
         columns_kernel,
         (strips, corners, from_left, from_right, part, rows),
         (((2, half, LANES), F32),),
-        "columns",
         8,
         (pltpu.VMEM((len(NAMES) + 3, 2, pairs + 32, LANES), F32),),
         4_000_000,
     )
     count = lax.axis_size("row")
     if count == 4:
-        one, three, two = (shifted(mine, "row", by) for by in (1, 3, 2))
-        coarse_sums = (mine + two) + (one + three)
+        theirs = {}
+        for other in (1, 2, 3):
+            theirs[other] = lax.ppermute(mine, "row", [(i, i ^ other) for i in range(count)])
+        coarse_sums = (mine + theirs[2]) + (theirs[1] + theirs[3])
     else:
         coarse_sums = lax.psum(mine, "row")
     averages = coarse_sums * jnp.float32(1.0 / (reals * count * BLOCK * BLOCK))
@@ -499,6 +475,4 @@
 def solution(mesh):
     in_specs = (P("row", "gx", "gy"), P(None, "row", "gx", "gy"))
     out_specs = (P("gx", "gy"), P("gx", "gy"))
-    return jax.shard_map(
-        per_device, mesh=mesh, in_specs=in_specs, out_specs=out_specs, check_vma=False
-    )
+    return jax.shard_map(integrated, mesh=mesh, in_specs=in_specs, out_specs=out_specs, check_vma=False)

time: 24.4 us -> 22.9 us (0.939)
  Pallas kernels: 8.86 us -> 7.59 us
    ppermute x6 -> x3, starting transfers between devices: 8.72 us -> 4.05 us  [shifted(): lax.ppermute(value, axis, [(i, (i + by) % count) for i in range(count)])]
    ppermute x0 -> x3, starting transfers between devices: none -> 4.45 us  [integrated(): lax.ppermute(mine, 'row', [(i, i ^ other) for i in range(count)])]
    ppermute x6 -> x3, waiting for transfers between devices: 5.37 us -> 0.98 us  [shifted(): lax.ppermute(value, axis, [(i, (i + by) % count) for i in range(count)])]
    ppermute x0 -> x3, waiting for transfers between devices: none -> 4.38 us  [integrated(): lax.ppermute(mine, 'row', [(i, i ^ other) for i in range(count)])]
    pallas_call x5, Pallas kernels: 8.86 us -> 7.59 us  [call(): pl.pallas_call(kernel, out_shape=tuple((pltpu.VMEM(shape, dtype) for shap...]
  transfers between devices with their start and end apart: 6 -> 6, of which waited for: 4 -> 5; matrix products, arithmetic and copies ran while one was open for 0% -> 0% of each run, Pallas kernels for 28% -> 24%
where the time goes in v3:
time: 22.9 us; the launch traced here: 22.8 us
  starting transfers between devices  8.5 us (37%)
  Pallas kernels  7.59 us (33%)
  waiting for transfers between devices  5.36 us (23%)
  between operations  0.69 us (3%)
  other arithmetic  0.63 us (3%)
    pallas_call x5, Pallas kernels, call(): pl.pallas_call(kernel, out_shape=tuple((pltpu.VMEM(shape, dtype) for shap...  7.59 us
    ppermute x3, starting transfers between devices, integrated(): lax.ppermute(mine, 'row', [(i, i ^ other) for i in range(count)])  4.45 us
    ppermute x3, waiting for transfers between devices, integrated(): lax.ppermute(mine, 'row', [(i, i ^ other) for i in range(count)])  4.38 us
    ppermute x3, starting transfers between devices, shifted(): lax.ppermute(value, axis, [(i, (i + by) % count) for i in range(count)])  4.05 us
    ppermute x3, waiting for transfers between devices, shifted(): lax.ppermute(value, axis, [(i, (i + by) % count) for i in range(count)])  0.98 us
    add x1, other arithmetic, integrated(): projected = coverage + LEAP / 2.0 * (coverage - averages[0])  0.62 us
  transfers between devices with their start and end apart: 6, of which 5 were waited for; matrix products, arithmetic and copies ran while one was open for 0% of the time, Pallas kernels for 24%

profile of v3, /device:TPU:0, one launch (start us, length us, event | category | flops | bytes accessed | tf_op | source)
XLA Modules:
  0.0 22.8 jit_solution(9453688067123036400)
XLA Ops:
  0.6 0.0 copy-start
  0.6 0.0 copy-start.1
  0.6 1.4 %shard_map.42 = (bf16[8,4,8,128]{3,2,1,0:T(8,128)(2,1)S(1)}, bf16[8,4,8,128]{3,2,1,0:T(8,128)(2,1)S(1)}) custom-call(s32[8,128,512]{2,1,0:T(8,128)} %occ.3, bf16[4,8,128,512]{3,2,1,0:T(8,128)(2,1)} %draws.3), custom_call_target="tpu_custom_call" | custom-call | flops 1000000 | tf_op jit(solution)/shard_map/pallas_call | solution.py:387
  2.1 4.0 %collective-permute-start = (bf16[8,4,8,128]{3,2,1,0:T(8,128)(2,1)S(1)}, bf16[8,4,8,128]{3,2,1,0:T(8,128)(2,1)S(1)}, u32[]{:S(2)}, u32[]{:S(2)}) collective-permute-start(bf16[8,4,8,128]{3,2,1,0:T(8,128)(2,1)S(1)} %get-tuple-element.10), channel_id=1, source_target_pairs={{0,24},{8,0},{16,8},{24,16},{1,25},{9,1},{17,9},{25,17},{2,26},{10... | collective-permute-start | bytes 196616 | tf_op jit(solution)/shard_map/ppermute | solution.py:375
  6.1 0.0 collective-permute-start.1
  6.1 0.0 copy-done
  6.1 0.0 copy-done.1
  6.1 4.5 %shard_map.41 = (f32[6,8,2,4,8,128]{5,4,3,2,1,0:T(8,128)S(1)}, f32[6,2,64,128]{3,2,1,0:T(8,128)S(1)}, f32[2,32,128]{2,1,0:T(8,128)S(1)}) custom-call(s32[8,128,512]{2,1,0:T(8,128)S(1)} %copy-done.1, bf16[4,8,128,512]{3,2,1,0:T(8,128)(2,1)S(1)} %copy-done), custom_call_target="tpu_custom_call" | custom-call | flops 40000000 | tf_op jit(solution)/shard_map/pallas_call | solution.py:387
  10.6 0.0 collective-permute-done.below
  10.6 0.7 %collective-permute-done.1.above = bf16[8,4,8,128]{3,2,1,0:T(8,128)(2,1)S(1)} collective-permute-done((bf16[8,4,8,128]{3,2,1,0:T(8,128)(2,1)S(1)}, bf16[8,4,8,128]{3,2,1,0:T(8,128)(2,1)S(1)}, u32[]{:S(2)}, u32[]{:S(2)}) %collective-permute-start.1) | collective-permute-done | bytes 65568 | tf_op jit(solution)/shard_map/ppermute | solution.py:375
  11.2 0.1 shard_map.43
  11.3 0.1 collective-permute-start.2
  11.4 1.0 %shard_map.44.rows = f32[8,128]{1,0:T(8,128)S(1)} custom-call(bf16[8,4,8,128]{3,2,1,0:T(8,128)(2,1)S(1)} %collective-permute-done.below, bf16[8,4,8,128]{3,2,1,0:T(8,128)(2,1)S(1)} %collective-permute-done.1.above, f32[6,8,2,4,8,128]{5,4,3,2,1,0:T(8,128)S(1)} %get-tuple-element.15.frames), custom_call_target="tpu_custom_call" | custom-call | flops 10000000 | tf_op jit(solution)/shard_map/pallas_call | solution.py:387
  12.4 0.3 %collective-permute-done.2.from_left.from_right = bf16[336,128]{1,0:T(8,128)(2,1)S(1)} collective-permute-done((bf16[336,128]{1,0:T(8,128)(2,1)S(1)}, bf16[336,128]{1,0:T(8,128)(2,1)S(1)}, u32[]{:S(2)}, u32[]{:S(2)}) %collective-permute-start.2) | collective-permute-done | bytes 86048 | tf_op jit(solution)/shard_map/ppermute | solution.py:375
  12.7 0.6 %shard_map.45 = f32[2,32,128]{2,1,0:T(8,128)S(1)} custom-call(f32[6,2,64,128]{3,2,1,0:T(8,128)S(1)} %get-tuple-element.9.strips, f32[2,2,8,128]{3,2,1,0:T(8,128)S(1)} %get-tuple-element.12.corners, bf16[336,128]{1,0:T(8,128)(2,1)S(1)} %collective-permute-done.2.from_left.from_right, bf16[336,128]{1,0:T(8,128)(2,1)S(1)} %collective-permute-done.2.from_left.from_right, ...), custom_call_target="tpu_custom_call" | custom-call | flops 4000000 | tf_op jit(solution)/shard_map/pallas_call | solution.py:387
  13.3 3.7 %collective-permute-start.5 = (f32[2,32,128]{2,1,0:T(8,128)S(1)}, f32[2,32,128]{2,1,0:T(8,128)S(1)}, u32[]{:S(2)}, u32[]{:S(2)}) collective-permute-start(f32[2,32,128]{2,1,0:T(8,128)S(1)} %shard_map.45), channel_id=1, source_target_pairs={{0,3},{1,2},{2,1},{3,0},{4,7},{5,6},{6,5},{7,4},{8,11},{9,10},{10,... | collective-permute-start | bytes 98312 | tf_op jit(solution)/shard_map/ppermute | solution.py:465
  17.0 0.0 collective-permute-start.4
  17.0 0.8 %collective-permute-start.3 = (f32[2,32,128]{2,1,0:T(8,128)S(1)}, f32[2,32,128]{2,1,0:T(8,128)S(1)}, u32[]{:S(2)}, u32[]{:S(2)}) collective-permute-start(f32[2,32,128]{2,1,0:T(8,128)S(1)} %shard_map.45), channel_id=1, source_target_pairs={{0,2},{1,3},{2,0},{3,1},{4,6},{5,7},{6,4},{7,5},{8,10},{9,11},{10,... | collective-permute-start | bytes 98312 | tf_op jit(solution)/shard_map/ppermute | solution.py:465
  17.8 1.3 %collective-permute-done.5 = f32[2,32,128]{2,1,0:T(8,128)S(1)} collective-permute-done((f32[2,32,128]{2,1,0:T(8,128)S(1)}, f32[2,32,128]{2,1,0:T(8,128)S(1)}, u32[]{:S(2)}, u32[]{:S(2)}) %collective-permute-start.5) | collective-permute-done | bytes 32800 | tf_op jit(solution)/shard_map/ppermute | solution.py:465
  19.1 2.0 %collective-permute-done.4 = f32[2,32,128]{2,1,0:T(8,128)S(1)} collective-permute-done((f32[2,32,128]{2,1,0:T(8,128)S(1)}, f32[2,32,128]{2,1,0:T(8,128)S(1)}, u32[]{:S(2)}, u32[]{:S(2)}) %collective-permute-start.4) | collective-permute-done | bytes 32800 | tf_op jit(solution)/shard_map/ppermute | solution.py:465
  21.1 1.0 %collective-permute-done.3 = f32[2,32,128]{2,1,0:T(8,128)S(1)} collective-permute-done((f32[2,32,128]{2,1,0:T(8,128)S(1)}, f32[2,32,128]{2,1,0:T(8,128)S(1)}, u32[]{:S(2)}, u32[]{:S(2)}) %collective-permute-start.3) | collective-permute-done | bytes 32800 | tf_op jit(solution)/shard_map/ppermute | solution.py:465
  22.2 0.6 %fusion.2 = (f32[32,128]{1,0:T(8,128)}, f32[32,128]{1,0:T(8,128)}) fusion(f32[2,32,128]{2,1,0:T(8,128)S(1)} %add_multiply_fusion), kind=kLoop, calls=%fused_computation.4 | loop fusion | flops 12288 | bytes 65536 | tf_op jit(solution)/shard_map/add | solution.py:471
  (1 shorter events, 0.0 us)
Async XLA Ops:
  0.6 5.5 %copy-start = (bf16[4,8,128,512]{3,2,1,0:T(8,128)(2,1)S(1)}, bf16[4,8,128,512]{3,2,1,0:T(8,128)(2,1)}, u32[]{:S(2)}) copy-start(bf16[4,8,128,512]{3,2,1,0:T(8,128)(2,1)} %draws.3) | copy-start | bytes 12582916
  0.6 5.4 %copy-start.1 = (s32[8,128,512]{2,1,0:T(8,128)S(1)}, s32[8,128,512]{2,1,0:T(8,128)}, u32[]{:S(2)}) copy-start(s32[8,128,512]{2,1,0:T(8,128)} %occ.3) | copy-start | bytes 6291460
  2.1 8.5 %collective-permute-start = (bf16[8,4,8,128]{3,2,1,0:T(8,128)(2,1)S(1)}, bf16[8,4,8,128]{3,2,1,0:T(8,128)(2,1)S(1)}, u32[]{:S(2)}, u32[]{:S(2)}) collective-permute-start(bf16[8,4,8,128]{3,2,1,0:T(8,128)(2,1)S(1)} %get-tuple-element.10), channel_id=1, source_target_pairs={{0,24},{8,0},{16,8},{24,16},{1,25},{9,1},{17,9},{25,17},{2,26},{10... | collective-permute-start | bytes 196616 | tf_op jit(solution)/shard_map/ppermute | solution.py:375
  6.1 5.2 %collective-permute-start.1 = (bf16[8,4,8,128]{3,2,1,0:T(8,128)(2,1)S(1)}, bf16[8,4,8,128]{3,2,1,0:T(8,128)(2,1)S(1)}, u32[]{:S(2)}, u32[]{:S(2)}) collective-permute-start(bf16[8,4,8,128]{3,2,1,0:T(8,128)(2,1)S(1)} %get-tuple-element.11), channel_id=1, source_target_pairs={{0,8},{8,16},{16,24},{24,0},{1,9},{9,17},{17,25},{25,1},{2,10},{10... | collective-permute-start | bytes 196616 | tf_op jit(solution)/shard_map/ppermute | solution.py:375
  11.3 1.3 %collective-permute-start.2 = (bf16[336,128]{1,0:T(8,128)(2,1)S(1)}, bf16[336,128]{1,0:T(8,128)(2,1)S(1)}, u32[]{:S(2)}, u32[]{:S(2)}) collective-permute-start(bf16[336,128]{1,0:T(8,128)(2,1)S(1)} %get-tuple-element.13), channel_id=1, source_target_pairs={{0,4},{4,0},{1,5},{5,1},{2,6},{6,2},{3,7},{7,3},{8,12},{12,8},{9,1... | collective-permute-start | bytes 258056 | tf_op jit(solution)/shard_map/ppermute | solution.py:375
  13.3 5.8 %collective-permute-start.5 = (f32[2,32,128]{2,1,0:T(8,128)S(1)}, f32[2,32,128]{2,1,0:T(8,128)S(1)}, u32[]{:S(2)}, u32[]{:S(2)}) collective-permute-start(f32[2,32,128]{2,1,0:T(8,128)S(1)} %shard_map.45), channel_id=1, source_target_pairs={{0,3},{1,2},{2,1},{3,0},{4,7},{5,6},{6,5},{7,4},{8,11},{9,10},{10,... | collective-permute-start | bytes 98312 | tf_op jit(solution)/shard_map/ppermute | solution.py:465
  17.0 4.1 %collective-permute-start.4 = (f32[2,32,128]{2,1,0:T(8,128)S(1)}, f32[2,32,128]{2,1,0:T(8,128)S(1)}, u32[]{:S(2)}, u32[]{:S(2)}) collective-permute-start(f32[2,32,128]{2,1,0:T(8,128)S(1)} %shard_map.45), channel_id=1, source_target_pairs={{0,1},{1,0},{2,3},{3,2},{4,5},{5,4},{6,7},{7,6},{8,9},{9,8},{10,11... | collective-permute-start | bytes 98312 | tf_op jit(solution)/shard_map/ppermute | solution.py:465
  17.0 5.2 %collective-permute-start.3 = (f32[2,32,128]{2,1,0:T(8,128)S(1)}, f32[2,32,128]{2,1,0:T(8,128)S(1)}, u32[]{:S(2)}, u32[]{:S(2)}) collective-permute-start(f32[2,32,128]{2,1,0:T(8,128)S(1)} %shard_map.45), channel_id=1, source_target_pairs={{0,2},{1,3},{2,0},{3,1},{4,6},{5,7},{6,4},{7,5},{8,10},{9,11},{10,... | collective-permute-start | bytes 98312 | tf_op jit(solution)/shard_map/ppermute | solution.py:465

commit v4 on v3

--- a/solution.py
+++ b/solution.py
@@ -124,7 +124,7 @@
 NAMES = ("p0", "p1", "u0", "u1", "u2")
 
 
-def tile_kernel(occ, draws, frames, strips, part, natural, state, sums):
+def tile_kernel(occ, draws, frames, strips, sums, natural, state):
     reals, height, width = occ.shape
     pairs = height // 2
     tiles = width // LANES
@@ -136,11 +136,11 @@
     strips[...] = jnp.zeros_like(strips)
     for colour in range(2):
         for c in range(tiles):
-            state[colour, c, 0:8] = jnp.zeros((8, LANES), F32)
-            state[colour, c, pairs + 8 : pairs + 16] = jnp.zeros((8, LANES), F32)
-
-    @pl.loop(0, reals)
-    def _(r):
+            for i in range(2):
+                state[i, colour, c, 0:8] = jnp.zeros((8, LANES), F32)
+                state[i, colour, c, pairs + 8 : pairs + 16] = jnp.zeros((8, LANES), F32)
+
+    def one(r, natural, state):
         group = lane // GROUP == r
         from_left = group & (lane % GROUP >= BLOCK)
 
@@ -156,7 +156,7 @@
                 pltpu.store(strips.at[index, 1, rows], pltpu.roll(value, r * GROUP + 12, 1), mask=group)
 
         for c in range(tiles):
-            natural[sweeps, c] = occ[r, :, c * LANES : (c + 1) * LANES].astype(F32)
+            natural[sweeps, c, :height] = occ[r, :, c * LANES : (c + 1) * LANES].astype(F32)
         for start in range(0, pairs, CHUNK):
             for c in range(tiles):
                 first = natural[sweeps, c, pl.ds(2 * start, CHUNK, stride=2)]
@@ -171,7 +171,7 @@
             colour = w % 2
             other = 1 - colour
             for c in range(tiles):
-                natural[w, c] = draws[w, r, :, c * LANES : (c + 1) * LANES].astype(F32)
+                natural[w, c, :height] = draws[w, r, :, c * LANES : (c + 1) * LANES].astype(F32)
             for start in range(0, pairs, CHUNK):
                 heres = [state[other, c, 8 + start : 8 + start + CHUNK] for c in range(tiles)]
                 for c in range(tiles):
@@ -194,18 +194,12 @@
                         snapshot = 0 if w == sweeps - 3 else 1
                         sums[snapshot, c, start : start + CHUNK] += here + new
 
-    half = pairs // 2
-    total = jnp.zeros((2 * half, LANES), F32)
-    for c in range(tiles):
-        rows = jnp.concatenate(
-            [
-                sums[s, c, pl.ds(0, half, stride=2)] + sums[s, c, pl.ds(1, half, stride=2)]
-                for s in range(2)
-            ]
-        )
-        total += selected(rows, fold_lanes(c * (LANES // BLOCK)))
-    part[0] = total[:half]
-    part[1] = total[half:]
+    together = 2 if reals % 2 == 0 else 1
+
+    @pl.loop(0, reals // together)
+    def _(step):
+        for i in range(together):
+            one(step * together + i, natural.at[i], state.at[i])
 
 
 def strips_kernel(below, above, strips, message, corners):
@@ -232,7 +226,7 @@
         ).astype(BF16)
 
 
-def rows_kernel(below, above, frames, out, arrays):
+def rows_kernel(below, above, frames, inner, out, arrays):
     reals, tiles = below.shape[:2]
     sweeps = frames.shape[0] - 2
     even = even_lanes((8, LANES))
@@ -272,22 +266,22 @@
                         both = here + new
                         before = sums[s][side][c]
                         sums[s][side][c] = both if before is None else before + both
-    total = jnp.zeros((8, LANES), F32)
+    half = inner.shape[2] // 2
+    total = jnp.zeros((2 * half, LANES), F32)
     for c in range(tiles):
-        rows = jnp.zeros((8, LANES), F32)
+        lines = []
         for s in range(2):
-            for side in sides:
-                both = sums[s][side][c]
-                both = both + pltpu.roll(both, 1, 0)
-                index = 2 * s + side
-                shift = (index - (1 if side == 0 else 7)) % 8
-                both = both if shift == 0 else pltpu.roll(both, shift, 0)
-                rows = jnp.where(row == index, both, rows)
-        total += selected(rows, fold_lanes(c * (LANES // BLOCK)))
-    out[...] = total
-
-
-def columns_kernel(strips, corners, from_left, from_right, part, rows, out, arrays):
+            cells = inner[s, c, pl.ds(0, half, stride=2)] + inner[s, c, pl.ds(1, half, stride=2)]
+            top, bottom = sums[s][0][c], sums[s][1][c]
+            lines.append(jnp.where(row == 0, top + pltpu.roll(top, 7, 0), cells[:8]))
+            lines.append(cells[8 : half - 8])
+            lines.append(jnp.where(row == 7, bottom + pltpu.roll(bottom, 1, 0), cells[half - 8 :]))
+        total += selected(jnp.concatenate(lines), fold_lanes(c * (LANES // BLOCK)))
+    out[0] = total[:half]
+    out[1] = total[half:]
+
+
+def columns_kernel(strips, corners, from_left, from_right, part, out, arrays):
     pairs = strips.shape[2]
     sweeps = strips.shape[0] - 2
     base = 16
@@ -344,28 +338,20 @@
             if w == sweeps - 3 or w == sweeps - 1:
                 s = 0 if w == sweeps - 3 else 1
                 arrays[count + 1 + s, side, base : base + pairs] = (here + new)[grow : grow + pairs]
-    source = iota((LANES, LANES), 0) % GROUP
-    target = iota((LANES, LANES), 1)
-    total = jnp.zeros((2 * half, LANES), F32)
-    for side in range(2):
-        rows_of = jnp.concatenate(
-            [
+    column = iota((half, LANES), 1)
+    group = column % GROUP
+    for s in range(2):
+        value = part[s]
+        for side in range(2):
+            cells = (
                 arrays[count + 1 + s, side, pl.ds(base, half, stride=2)]
                 + arrays[count + 1 + s, side, pl.ds(base + 1, half, stride=2)]
-                for s in range(2)
-            ]
-        )
-        first = BLOCK if side == 0 else 2 * BLOCK
-        pick = (source >= first) & (source < first + BLOCK) & (target == (0 if side == 0 else LANES - 1))
-        total += selected(rows_of, selection(pick))
-    row = iota((half, LANES), 0)
-    column = iota((half, LANES), 1)
-    for s in range(2):
-        value = part[s]
-        value = jnp.where(row == 0, rows[2 * s : 2 * s + 1], value)
-        value = jnp.where(row == half - 1, rows[2 * s + 1 : 2 * s + 2], value)
-        edge = (column == 0) | (column == LANES - 1)
-        out[s] = jnp.where(edge, total[s * half : (s + 1) * half], value)
+            )
+            first = BLOCK if side == 0 else 2 * BLOCK
+            own = jnp.where((group >= first) & (group < first + BLOCK), cells, 0.0)
+            sums = jnp.sum(own, axis=1, keepdims=True)
+            value = jnp.where(column == (0 if side == 0 else LANES - 1), sums, value)
+        out[s] = value
 
 
 def shifted(value, axis, by):
@@ -414,19 +400,18 @@
         pltpu.HBM,
     )
     below, above = both_ways(low, high, "gx")
-    frames, strips, part = call(
+    frames, strips, inner = call(
         tile_kernel,
         (occupancy, random_draws),
         (
             ((2 + sweeps, reals, 2, tiles, 8, LANES), F32),
             ((2 + sweeps, 2, pairs, LANES), F32),
-            ((2, half, LANES), F32),
+            ((2, tiles, pairs, LANES), F32),
         ),
         24,
         (
-            pltpu.VMEM((sweeps + 1, tiles, height, LANES), F32),
-            pltpu.VMEM((2, tiles, pairs + 16, LANES), F32),
-            pltpu.VMEM((2, tiles, pairs, LANES), F32),
+            pltpu.VMEM((2, sweeps + 1, tiles, height + 8, LANES), F32),
+            pltpu.VMEM((2, 2, tiles, pairs + 16, LANES), F32),
         ),
         40_000_000,
     )
@@ -442,17 +427,17 @@
         from_left = from_right = shifted(message, "gy", 1)
     else:
         from_right, from_left = both_ways(message, message, "gy")
-    (rows,) = call(
+    (part,) = call(
         rows_kernel,
-        (below, above, frames),
-        (((8, LANES), F32),),
+        (below, above, frames, inner),
+        (((2, half, LANES), F32),),
         8,
         (pltpu.VMEM((len(NAMES), reals, 2, tiles, 8, LANES), F32),),
         10_000_000,
     )
     (mine,) = call(
         columns_kernel,
-        (strips, corners, from_left, from_right, part, rows),
+        (strips, corners, from_left, from_right, part),
         (((2, half, LANES), F32),),
         8,
         (pltpu.VMEM((len(NAMES) + 3, 2, pairs + 32, LANES), F32),),

time: 22.9 us -> 22.9 us (level)
  Pallas kernels: 7.59 us -> 7.2 us
  waiting for transfers between devices: 5.36 us -> 5.68 us
    pallas_call x5, Pallas kernels: 7.59 us -> 7.2 us  [call(): pl.pallas_call(kernel, out_shape=tuple((pltpu.VMEM(shape, dtype) for shap...]
    ppermute x3, waiting for transfers between devices: 0.98 us -> 1.3 us  [shifted(): lax.ppermute(value, axis, [(i, (i + by) % count) for i in range(count)])]
  transfers between devices with their start and end apart: 6 -> 6, of which waited for: 5 -> 5; matrix products, arithmetic and copies ran while one was open for 0% -> 0% of each run, Pallas kernels for 24% -> 22%
where the time goes in v4:
time: 22.9 us; the launch traced here: 22.7 us
  starting transfers between devices  8.48 us (37%)
  Pallas kernels  7.2 us (31%)
  waiting for transfers between devices  5.68 us (25%)
  between operations  0.7 us (3%)
  other arithmetic  0.63 us (3%)
    pallas_call x5, Pallas kernels, call(): pl.pallas_call(kernel, out_shape=tuple((pltpu.VMEM(shape, dtype) for shap...  7.2 us
    ppermute x3, starting transfers between devices, integrated(): lax.ppermute(mine, 'row', [(i, i ^ other) for i in range(count)])  4.43 us
    ppermute x3, waiting for transfers between devices, integrated(): lax.ppermute(mine, 'row', [(i, i ^ other) for i in range(count)])  4.38 us
    ppermute x3, starting transfers between devices, shifted(): lax.ppermute(value, axis, [(i, (i + by) % count) for i in range(count)])  4.05 us
    ppermute x3, waiting for transfers between devices, shifted(): lax.ppermute(value, axis, [(i, (i + by) % count) for i in range(count)])  1.3 us
    add x1, other arithmetic, integrated(): projected = coverage + LEAP / 2.0 * (coverage - averages[0])  0.62 us
  transfers between devices with their start and end apart: 6, of which 5 were waited for; matrix products, arithmetic and copies ran while one was open for 0% of the time, Pallas kernels for 22%

profile of v4, /device:TPU:0, one launch (start us, length us, event | category | flops | bytes accessed | tf_op | source)
XLA Modules:
  0.0 22.7 jit_solution(6156038105004949548)
XLA Ops:
  0.6 0.0 copy-start
  0.6 0.0 copy-start.1
  0.6 1.4 %shard_map.42 = (bf16[8,4,8,128]{3,2,1,0:T(8,128)(2,1)S(1)}, bf16[8,4,8,128]{3,2,1,0:T(8,128)(2,1)S(1)}) custom-call(s32[8,128,512]{2,1,0:T(8,128)} %occ.3, bf16[4,8,128,512]{3,2,1,0:T(8,128)(2,1)} %draws.3), custom_call_target="tpu_custom_call" | custom-call | flops 1000000 | tf_op jit(solution)/shard_map/pallas_call | solution.py:373
  2.1 4.0 %collective-permute-start = (bf16[8,4,8,128]{3,2,1,0:T(8,128)(2,1)S(1)}, bf16[8,4,8,128]{3,2,1,0:T(8,128)(2,1)S(1)}, u32[]{:S(2)}, u32[]{:S(2)}) collective-permute-start(bf16[8,4,8,128]{3,2,1,0:T(8,128)(2,1)S(1)} %get-tuple-element.10), channel_id=1, source_target_pairs={{0,24},{8,0},{16,8},{24,16},{1,25},{9,1},{17,9},{25,17},{2,26},{10... | collective-permute-start | bytes 196616 | tf_op jit(solution)/shard_map/ppermute | solution.py:361
  6.1 0.0 collective-permute-start.1
  6.1 0.0 copy-done
  6.1 0.0 copy-done.1
  6.1 4.1 %shard_map.41 = (f32[6,8,2,4,8,128]{5,4,3,2,1,0:T(8,128)S(1)}, f32[6,2,64,128]{3,2,1,0:T(8,128)S(1)}, f32[2,4,64,128]{3,2,1,0:T(8,128)S(1)}) custom-call(s32[8,128,512]{2,1,0:T(8,128)S(1)} %copy-done.1, bf16[4,8,128,512]{3,2,1,0:T(8,128)(2,1)S(1)} %copy-done), custom_call_target="tpu_custom_call" | custom-call | flops 40000000 | tf_op jit(solution)/shard_map/pallas_call | solution.py:373
  10.2 0.0 collective-permute-done.below
  10.2 1.0 %collective-permute-done.1.above = bf16[8,4,8,128]{3,2,1,0:T(8,128)(2,1)S(1)} collective-permute-done((bf16[8,4,8,128]{3,2,1,0:T(8,128)(2,1)S(1)}, bf16[8,4,8,128]{3,2,1,0:T(8,128)(2,1)S(1)}, u32[]{:S(2)}, u32[]{:S(2)}) %collective-permute-start.1) | collective-permute-done | bytes 65568 | tf_op jit(solution)/shard_map/ppermute | solution.py:361
  11.2 0.1 shard_map.43
  11.3 0.1 collective-permute-start.2
  11.4 1.0 %shard_map.44.part = f32[2,32,128]{2,1,0:T(8,128)S(1)} custom-call(bf16[8,4,8,128]{3,2,1,0:T(8,128)(2,1)S(1)} %collective-permute-done.below, bf16[8,4,8,128]{3,2,1,0:T(8,128)(2,1)S(1)} %collective-permute-done.1.above, f32[6,8,2,4,8,128]{5,4,3,2,1,0:T(8,128)S(1)} %get-tuple-element.14.frames, f32[2,4,64,128]{3,2,1,0:T(8,128)S(1)} %get-tuple-element.15.inner), custom_call_target="tpu_custom_call" | custom-call | flops 10000000 | tf_op jit(solution)/shard_map/pallas_call | solution.py:373
  12.4 0.3 %collective-permute-done.2.from_left.from_right = bf16[336,128]{1,0:T(8,128)(2,1)S(1)} collective-permute-done((bf16[336,128]{1,0:T(8,128)(2,1)S(1)}, bf16[336,128]{1,0:T(8,128)(2,1)S(1)}, u32[]{:S(2)}, u32[]{:S(2)}) %collective-permute-start.2) | collective-permute-done | bytes 86048 | tf_op jit(solution)/shard_map/ppermute | solution.py:361
  12.7 0.6 %shard_map.45 = f32[2,32,128]{2,1,0:T(8,128)S(1)} custom-call(f32[6,2,64,128]{3,2,1,0:T(8,128)S(1)} %get-tuple-element.9.strips, f32[2,2,8,128]{3,2,1,0:T(8,128)S(1)} %get-tuple-element.12.corners, bf16[336,128]{1,0:T(8,128)(2,1)S(1)} %collective-permute-done.2.from_left.from_right, bf16[336,128]{1,0:T(8,128)(2,1)S(1)} %collective-permute-done.2.from_left.from_right, ...), custom_call_target="tpu_custom_call" | custom-call | flops 4000000 | tf_op jit(solution)/shard_map/pallas_call | solution.py:373
  13.3 3.6 %collective-permute-start.5 = (f32[2,32,128]{2,1,0:T(8,128)S(1)}, f32[2,32,128]{2,1,0:T(8,128)S(1)}, u32[]{:S(2)}, u32[]{:S(2)}) collective-permute-start(f32[2,32,128]{2,1,0:T(8,128)S(1)} %shard_map.45), channel_id=1, source_target_pairs={{0,3},{1,2},{2,1},{3,0},{4,7},{5,6},{6,5},{7,4},{8,11},{9,10},{10,... | collective-permute-start | bytes 98312 | tf_op jit(solution)/shard_map/ppermute | solution.py:450
  16.9 0.0 collective-permute-start.4
  16.9 0.8 %collective-permute-start.3 = (f32[2,32,128]{2,1,0:T(8,128)S(1)}, f32[2,32,128]{2,1,0:T(8,128)S(1)}, u32[]{:S(2)}, u32[]{:S(2)}) collective-permute-start(f32[2,32,128]{2,1,0:T(8,128)S(1)} %shard_map.45), channel_id=1, source_target_pairs={{0,2},{1,3},{2,0},{3,1},{4,6},{5,7},{6,4},{7,5},{8,10},{9,11},{10,... | collective-permute-start | bytes 98312 | tf_op jit(solution)/shard_map/ppermute | solution.py:450
  17.7 1.4 %collective-permute-done.5 = f32[2,32,128]{2,1,0:T(8,128)S(1)} collective-permute-done((f32[2,32,128]{2,1,0:T(8,128)S(1)}, f32[2,32,128]{2,1,0:T(8,128)S(1)}, u32[]{:S(2)}, u32[]{:S(2)}) %collective-permute-start.5) | collective-permute-done | bytes 32800 | tf_op jit(solution)/shard_map/ppermute | solution.py:450
  19.1 2.0 %collective-permute-done.4 = f32[2,32,128]{2,1,0:T(8,128)S(1)} collective-permute-done((f32[2,32,128]{2,1,0:T(8,128)S(1)}, f32[2,32,128]{2,1,0:T(8,128)S(1)}, u32[]{:S(2)}, u32[]{:S(2)}) %collective-permute-start.4) | collective-permute-done | bytes 32800 | tf_op jit(solution)/shard_map/ppermute | solution.py:450
  21.1 1.0 %collective-permute-done.3 = f32[2,32,128]{2,1,0:T(8,128)S(1)} collective-permute-done((f32[2,32,128]{2,1,0:T(8,128)S(1)}, f32[2,32,128]{2,1,0:T(8,128)S(1)}, u32[]{:S(2)}, u32[]{:S(2)}) %collective-permute-start.3) | collective-permute-done | bytes 32800 | tf_op jit(solution)/shard_map/ppermute | solution.py:450
  22.1 0.6 %fusion.2 = (f32[32,128]{1,0:T(8,128)}, f32[32,128]{1,0:T(8,128)}) fusion(f32[2,32,128]{2,1,0:T(8,128)S(1)} %add_multiply_fusion), kind=kLoop, calls=%fused_computation.4 | loop fusion | flops 12288 | bytes 65536 | tf_op jit(solution)/shard_map/add | solution.py:456
  (1 shorter events, 0.0 us)
Async XLA Ops:
  0.6 5.5 %copy-start = (bf16[4,8,128,512]{3,2,1,0:T(8,128)(2,1)S(1)}, bf16[4,8,128,512]{3,2,1,0:T(8,128)(2,1)}, u32[]{:S(2)}) copy-start(bf16[4,8,128,512]{3,2,1,0:T(8,128)(2,1)} %draws.3) | copy-start | bytes 12582916
  0.6 5.4 %copy-start.1 = (s32[8,128,512]{2,1,0:T(8,128)S(1)}, s32[8,128,512]{2,1,0:T(8,128)}, u32[]{:S(2)}) copy-start(s32[8,128,512]{2,1,0:T(8,128)} %occ.3) | copy-start | bytes 6291460
  2.1 8.1 %collective-permute-start = (bf16[8,4,8,128]{3,2,1,0:T(8,128)(2,1)S(1)}, bf16[8,4,8,128]{3,2,1,0:T(8,128)(2,1)S(1)}, u32[]{:S(2)}, u32[]{:S(2)}) collective-permute-start(bf16[8,4,8,128]{3,2,1,0:T(8,128)(2,1)S(1)} %get-tuple-element.10), channel_id=1, source_target_pairs={{0,24},{8,0},{16,8},{24,16},{1,25},{9,1},{17,9},{25,17},{2,26},{10... | collective-permute-start | bytes 196616 | tf_op jit(solution)/shard_map/ppermute | solution.py:361
  6.1 5.2 %collective-permute-start.1 = (bf16[8,4,8,128]{3,2,1,0:T(8,128)(2,1)S(1)}, bf16[8,4,8,128]{3,2,1,0:T(8,128)(2,1)S(1)}, u32[]{:S(2)}, u32[]{:S(2)}) collective-permute-start(bf16[8,4,8,128]{3,2,1,0:T(8,128)(2,1)S(1)} %get-tuple-element.11), channel_id=1, source_target_pairs={{0,8},{8,16},{16,24},{24,0},{1,9},{9,17},{17,25},{25,1},{2,10},{10... | collective-permute-start | bytes 196616 | tf_op jit(solution)/shard_map/ppermute | solution.py:361
  11.3 1.3 %collective-permute-start.2 = (bf16[336,128]{1,0:T(8,128)(2,1)S(1)}, bf16[336,128]{1,0:T(8,128)(2,1)S(1)}, u32[]{:S(2)}, u32[]{:S(2)}) collective-permute-start(bf16[336,128]{1,0:T(8,128)(2,1)S(1)} %get-tuple-element.13), channel_id=1, source_target_pairs={{0,4},{4,0},{1,5},{5,1},{2,6},{6,2},{3,7},{7,3},{8,12},{12,8},{9,1... | collective-permute-start | bytes 258056 | tf_op jit(solution)/shard_map/ppermute | solution.py:361
  13.3 5.8 %collective-permute-start.5 = (f32[2,32,128]{2,1,0:T(8,128)S(1)}, f32[2,32,128]{2,1,0:T(8,128)S(1)}, u32[]{:S(2)}, u32[]{:S(2)}) collective-permute-start(f32[2,32,128]{2,1,0:T(8,128)S(1)} %shard_map.45), channel_id=1, source_target_pairs={{0,3},{1,2},{2,1},{3,0},{4,7},{5,6},{6,5},{7,4},{8,11},{9,10},{10,... | collective-permute-start | bytes 98312 | tf_op jit(solution)/shard_map/ppermute | solution.py:450
  16.9 4.2 %collective-permute-start.4 = (f32[2,32,128]{2,1,0:T(8,128)S(1)}, f32[2,32,128]{2,1,0:T(8,128)S(1)}, u32[]{:S(2)}, u32[]{:S(2)}) collective-permute-start(f32[2,32,128]{2,1,0:T(8,128)S(1)} %shard_map.45), channel_id=1, source_target_pairs={{0,1},{1,0},{2,3},{3,2},{4,5},{5,4},{6,7},{7,6},{8,9},{9,8},{10,11... | collective-permute-start | bytes 98312 | tf_op jit(solution)/shard_map/ppermute | solution.py:450
  16.9 5.2 %collective-permute-start.3 = (f32[2,32,128]{2,1,0:T(8,128)S(1)}, f32[2,32,128]{2,1,0:T(8,128)S(1)}, u32[]{:S(2)}, u32[]{:S(2)}) collective-permute-start(f32[2,32,128]{2,1,0:T(8,128)S(1)} %shard_map.45), channel_id=1, source_target_pairs={{0,2},{1,3},{2,0},{3,1},{4,6},{5,7},{6,4},{7,5},{8,10},{9,11},{10,... | collective-permute-start | bytes 98312 | tf_op jit(solution)/shard_map/ppermute | solution.py:450

commit v5 on v4

--- a/solution.py
+++ b/solution.py
@@ -379,6 +379,9 @@
         compiler_params=pltpu.CompilerParams(vmem_limit_bytes=vmem * MIB),
         cost_estimate=pl.CostEstimate(flops=flops, bytes_accessed=0, transcendentals=0),
     )(*args)
+
+
+ROW_STEPS = ((2, 3, 1, 0), (3, 2, 0, 1), (1, 0, 3, 2))
 
 
 def integrated(occupancy, random_draws):
@@ -444,11 +447,13 @@
         4_000_000,
     )
     count = lax.axis_size("row")
-    if count == 4:
-        theirs = {}
-        for other in (1, 2, 3):
-            theirs[other] = lax.ppermute(mine, "row", [(i, i ^ other) for i in range(count)])
-        coarse_sums = (mine + theirs[2]) + (theirs[1] + theirs[3])
+    if count == len(ROW_STEPS) + 1:
+        theirs = []
+        for targets in ROW_STEPS:
+            theirs.append(lax.ppermute(mine, "row", list(enumerate(targets))))
+        swapped = [all(t[t[i]] == i for i in range(count)) for t in ROW_STEPS].index(True)
+        partner = theirs.pop(swapped)
+        coarse_sums = (mine + partner) + (theirs[0] + theirs[1])
     else:
         coarse_sums = lax.psum(mine, "row")
     averages = coarse_sums * jnp.float32(1.0 / (reals * count * BLOCK * BLOCK))

time: 22.9 us -> 23.4 us (1.022)
  waiting for transfers between devices: 5.68 us -> 6.11 us
    ppermute x3, waiting for transfers between devices: 4.38 us -> 4.81 us  [integrated(): theirs.append(lax.ppermute(mine, 'row', list(enumerate(targets))))]
  transfers between devices with their start and end apart: 6 -> 6, of which waited for: 5 -> 4; matrix products, arithmetic and copies ran while one was open for 0% -> 0% of each run, Pallas kernels for 22% -> 22%
where the time goes in v5:
time: 23.4 us; the launch traced here: 23.2 us
  starting transfers between devices  8.58 us (37%)
  Pallas kernels  7.2 us (31%)
  waiting for transfers between devices  6.11 us (26%)
  between operations  0.7 us (3%)
  other arithmetic  0.63 us (3%)
    pallas_call x5, Pallas kernels, call(): pl.pallas_call(kernel, out_shape=tuple((pltpu.VMEM(shape, dtype) for shap...  7.2 us
    ppermute x3, waiting for transfers between devices, integrated(): theirs.append(lax.ppermute(mine, 'row', list(enumerate(targets))))  4.81 us
    ppermute x3, starting transfers between devices, integrated(): theirs.append(lax.ppermute(mine, 'row', list(enumerate(targets))))  4.53 us
    ppermute x3, starting transfers between devices, shifted(): lax.ppermute(value, axis, [(i, (i + by) % count) for i in range(count)])  4.05 us
    ppermute x3, waiting for transfers between devices, shifted(): lax.ppermute(value, axis, [(i, (i + by) % count) for i in range(count)])  1.3 us
    add x1, other arithmetic, integrated(): projected = coverage + LEAP / 2.0 * (coverage - averages[0])  0.62 us
  transfers between devices with their start and end apart: 6, of which 4 were waited for; matrix products, arithmetic and copies ran while one was open for 0% of the time, Pallas kernels for 22%

profile of v5, /device:TPU:0, one launch (start us, length us, event | category | flops | bytes accessed | tf_op | source)
XLA Modules:
  0.0 23.2 jit_solution(132432413682368145)
XLA Ops:
  0.6 0.0 copy-start
  0.6 0.0 copy-start.1
  0.6 1.4 %shard_map.42 = (bf16[8,4,8,128]{3,2,1,0:T(8,128)(2,1)S(1)}, bf16[8,4,8,128]{3,2,1,0:T(8,128)(2,1)S(1)}) custom-call(s32[8,128,512]{2,1,0:T(8,128)} %occ.3, bf16[4,8,128,512]{3,2,1,0:T(8,128)(2,1)} %draws.3), custom_call_target="tpu_custom_call" | custom-call | flops 1000000 | tf_op jit(solution)/shard_map/pallas_call | solution.py:373
  2.1 4.0 %collective-permute-start = (bf16[8,4,8,128]{3,2,1,0:T(8,128)(2,1)S(1)}, bf16[8,4,8,128]{3,2,1,0:T(8,128)(2,1)S(1)}, u32[]{:S(2)}, u32[]{:S(2)}) collective-permute-start(bf16[8,4,8,128]{3,2,1,0:T(8,128)(2,1)S(1)} %get-tuple-element.10), channel_id=1, source_target_pairs={{0,24},{8,0},{16,8},{24,16},{1,25},{9,1},{17,9},{25,17},{2,26},{10... | collective-permute-start | bytes 196616 | tf_op jit(solution)/shard_map/ppermute | solution.py:361
  6.1 0.0 collective-permute-start.1
  6.1 0.0 copy-done
  6.1 0.0 copy-done.1
  6.1 4.1 %shard_map.41 = (f32[6,8,2,4,8,128]{5,4,3,2,1,0:T(8,128)S(1)}, f32[6,2,64,128]{3,2,1,0:T(8,128)S(1)}, f32[2,4,64,128]{3,2,1,0:T(8,128)S(1)}) custom-call(s32[8,128,512]{2,1,0:T(8,128)S(1)} %copy-done.1, bf16[4,8,128,512]{3,2,1,0:T(8,128)(2,1)S(1)} %copy-done), custom_call_target="tpu_custom_call" | custom-call | flops 40000000 | tf_op jit(solution)/shard_map/pallas_call | solution.py:373
  10.2 0.0 collective-permute-done.below
  10.2 1.0 %collective-permute-done.1.above = bf16[8,4,8,128]{3,2,1,0:T(8,128)(2,1)S(1)} collective-permute-done((bf16[8,4,8,128]{3,2,1,0:T(8,128)(2,1)S(1)}, bf16[8,4,8,128]{3,2,1,0:T(8,128)(2,1)S(1)}, u32[]{:S(2)}, u32[]{:S(2)}) %collective-permute-start.1) | collective-permute-done | bytes 65568 | tf_op jit(solution)/shard_map/ppermute | solution.py:361
  11.2 0.1 shard_map.43
  11.3 0.1 collective-permute-start.2
  11.4 1.0 %shard_map.44.part = f32[2,32,128]{2,1,0:T(8,128)S(1)} custom-call(bf16[8,4,8,128]{3,2,1,0:T(8,128)(2,1)S(1)} %collective-permute-done.below, bf16[8,4,8,128]{3,2,1,0:T(8,128)(2,1)S(1)} %collective-permute-done.1.above, f32[6,8,2,4,8,128]{5,4,3,2,1,0:T(8,128)S(1)} %get-tuple-element.14.frames, f32[2,4,64,128]{3,2,1,0:T(8,128)S(1)} %get-tuple-element.15.inner), custom_call_target="tpu_custom_call" | custom-call | flops 10000000 | tf_op jit(solution)/shard_map/pallas_call | solution.py:373
  12.4 0.3 %collective-permute-done.2.from_left.from_right = bf16[336,128]{1,0:T(8,128)(2,1)S(1)} collective-permute-done((bf16[336,128]{1,0:T(8,128)(2,1)S(1)}, bf16[336,128]{1,0:T(8,128)(2,1)S(1)}, u32[]{:S(2)}, u32[]{:S(2)}) %collective-permute-start.2) | collective-permute-done | bytes 86048 | tf_op jit(solution)/shard_map/ppermute | solution.py:361
  12.7 0.6 %shard_map.45 = f32[2,32,128]{2,1,0:T(8,128)S(1)} custom-call(f32[6,2,64,128]{3,2,1,0:T(8,128)S(1)} %get-tuple-element.9.strips, f32[2,2,8,128]{3,2,1,0:T(8,128)S(1)} %get-tuple-element.12.corners, bf16[336,128]{1,0:T(8,128)(2,1)S(1)} %collective-permute-done.2.from_left.from_right, bf16[336,128]{1,0:T(8,128)(2,1)S(1)} %collective-permute-done.2.from_left.from_right, ...), custom_call_target="tpu_custom_call" | custom-call | flops 4000000 | tf_op jit(solution)/shard_map/pallas_call | solution.py:373
  13.3 3.6 %collective-permute-start.5 = (f32[2,32,128]{2,1,0:T(8,128)S(1)}, f32[2,32,128]{2,1,0:T(8,128)S(1)}, u32[]{:S(2)}, u32[]{:S(2)}) collective-permute-start(f32[2,32,128]{2,1,0:T(8,128)S(1)} %shard_map.45), channel_id=1, source_target_pairs={{0,3},{1,2},{2,0},{3,1},{4,7},{5,6},{6,4},{7,5},{8,11},{9,10},{10,... | collective-permute-start | bytes 98312 | tf_op jit(solution)/shard_map/ppermute | solution.py:453
  16.9 0.0 collective-permute-start.4
  16.9 0.9 %collective-permute-start.3 = (f32[2,32,128]{2,1,0:T(8,128)S(1)}, f32[2,32,128]{2,1,0:T(8,128)S(1)}, u32[]{:S(2)}, u32[]{:S(2)}) collective-permute-start(f32[2,32,128]{2,1,0:T(8,128)S(1)} %shard_map.45), channel_id=1, source_target_pairs={{0,1},{1,0},{2,3},{3,2},{4,5},{5,4},{6,7},{7,6},{8,9},{9,8},{10,11... | collective-permute-start | bytes 98312 | tf_op jit(solution)/shard_map/ppermute | solution.py:453
  17.8 0.9 %collective-permute-done.5 = f32[2,32,128]{2,1,0:T(8,128)S(1)} collective-permute-done((f32[2,32,128]{2,1,0:T(8,128)S(1)}, f32[2,32,128]{2,1,0:T(8,128)S(1)}, u32[]{:S(2)}, u32[]{:S(2)}) %collective-permute-start.5) | collective-permute-done | bytes 32800 | tf_op jit(solution)/shard_map/ppermute | solution.py:453
  18.7 3.9 %collective-permute-done.4 = f32[2,32,128]{2,1,0:T(8,128)S(1)} collective-permute-done((f32[2,32,128]{2,1,0:T(8,128)S(1)}, f32[2,32,128]{2,1,0:T(8,128)S(1)}, u32[]{:S(2)}, u32[]{:S(2)}) %collective-permute-start.4) | collective-permute-done | bytes 32800 | tf_op jit(solution)/shard_map/ppermute | solution.py:453
  22.6 0.0 collective-permute-done.3
  22.6 0.6 %fusion.2 = (f32[32,128]{1,0:T(8,128)}, f32[32,128]{1,0:T(8,128)}) fusion(f32[2,32,128]{2,1,0:T(8,128)S(1)} %add_multiply_fusion), kind=kLoop, calls=%fused_computation.4 | loop fusion | flops 12288 | bytes 65536 | tf_op jit(solution)/shard_map/add | solution.py:461
  (1 shorter events, 0.0 us)
Async XLA Ops:
  0.6 5.5 %copy-start = (bf16[4,8,128,512]{3,2,1,0:T(8,128)(2,1)S(1)}, bf16[4,8,128,512]{3,2,1,0:T(8,128)(2,1)}, u32[]{:S(2)}) copy-start(bf16[4,8,128,512]{3,2,1,0:T(8,128)(2,1)} %draws.3) | copy-start | bytes 12582916
  0.6 5.4 %copy-start.1 = (s32[8,128,512]{2,1,0:T(8,128)S(1)}, s32[8,128,512]{2,1,0:T(8,128)}, u32[]{:S(2)}) copy-start(s32[8,128,512]{2,1,0:T(8,128)} %occ.3) | copy-start | bytes 6291460
  2.1 8.1 %collective-permute-start = (bf16[8,4,8,128]{3,2,1,0:T(8,128)(2,1)S(1)}, bf16[8,4,8,128]{3,2,1,0:T(8,128)(2,1)S(1)}, u32[]{:S(2)}, u32[]{:S(2)}) collective-permute-start(bf16[8,4,8,128]{3,2,1,0:T(8,128)(2,1)S(1)} %get-tuple-element.10), channel_id=1, source_target_pairs={{0,24},{8,0},{16,8},{24,16},{1,25},{9,1},{17,9},{25,17},{2,26},{10... | collective-permute-start | bytes 196616 | tf_op jit(solution)/shard_map/ppermute | solution.py:361
  6.1 5.2 %collective-permute-start.1 = (bf16[8,4,8,128]{3,2,1,0:T(8,128)(2,1)S(1)}, bf16[8,4,8,128]{3,2,1,0:T(8,128)(2,1)S(1)}, u32[]{:S(2)}, u32[]{:S(2)}) collective-permute-start(bf16[8,4,8,128]{3,2,1,0:T(8,128)(2,1)S(1)} %get-tuple-element.11), channel_id=1, source_target_pairs={{0,8},{8,16},{16,24},{24,0},{1,9},{9,17},{17,25},{25,1},{2,10},{10... | collective-permute-start | bytes 196616 | tf_op jit(solution)/shard_map/ppermute | solution.py:361
  11.3 1.3 %collective-permute-start.2 = (bf16[336,128]{1,0:T(8,128)(2,1)S(1)}, bf16[336,128]{1,0:T(8,128)(2,1)S(1)}, u32[]{:S(2)}, u32[]{:S(2)}) collective-permute-start(bf16[336,128]{1,0:T(8,128)(2,1)S(1)} %get-tuple-element.13), channel_id=1, source_target_pairs={{0,4},{4,0},{1,5},{5,1},{2,6},{6,2},{3,7},{7,3},{8,12},{12,8},{9,1... | collective-permute-start | bytes 258056 | tf_op jit(solution)/shard_map/ppermute | solution.py:361
  13.3 5.4 %collective-permute-start.5 = (f32[2,32,128]{2,1,0:T(8,128)S(1)}, f32[2,32,128]{2,1,0:T(8,128)S(1)}, u32[]{:S(2)}, u32[]{:S(2)}) collective-permute-start(f32[2,32,128]{2,1,0:T(8,128)S(1)} %shard_map.45), channel_id=1, source_target_pairs={{0,3},{1,2},{2,0},{3,1},{4,7},{5,6},{6,4},{7,5},{8,11},{9,10},{10,... | collective-permute-start | bytes 98312 | tf_op jit(solution)/shard_map/ppermute | solution.py:453
  16.9 5.7 %collective-permute-start.4 = (f32[2,32,128]{2,1,0:T(8,128)S(1)}, f32[2,32,128]{2,1,0:T(8,128)S(1)}, u32[]{:S(2)}, u32[]{:S(2)}) collective-permute-start(f32[2,32,128]{2,1,0:T(8,128)S(1)} %shard_map.45), channel_id=1, source_target_pairs={{0,2},{1,3},{2,1},{3,0},{4,6},{5,7},{6,5},{7,4},{8,10},{9,11},{10,... | collective-permute-start | bytes 98312 | tf_op jit(solution)/shard_map/ppermute | solution.py:453
  16.9 5.7 %collective-permute-start.3 = (f32[2,32,128]{2,1,0:T(8,128)S(1)}, f32[2,32,128]{2,1,0:T(8,128)S(1)}, u32[]{:S(2)}, u32[]{:S(2)}) collective-permute-start(f32[2,32,128]{2,1,0:T(8,128)S(1)} %shard_map.45), channel_id=1, source_target_pairs={{0,1},{1,0},{2,3},{3,2},{4,5},{5,4},{6,7},{7,6},{8,9},{9,8},{10,11... | collective-permute-start | bytes 98312 | tf_op jit(solution)/shard_map/ppermute | solution.py:453
